TPU v7x, 64 devices: a 2x2x8 block of a 4x4x8 slice. The times are simulated.
64 devices in a mesh: dp: 4 (over x, y), stage: 16 (over z, core).
Axes of the slice: x: 2, y: 2, z: 8, core: 2. Of those that a mesh axis runs over, the one named last changes fastest.
The devices are a block of a 4x4x8 slice.
Arguments:
- tokens: int32 [64, 64], P('dp'), parts along dimension 0
- labels: int32 [64, 64], P('dp'), parts along dimension 0
- emb_table: bfloat16 [30592, 128], replicated
- w_up: bfloat16 [16, 128, 512], P('stage')
- w_down: bfloat16 [16, 512, 128], P('stage')
Outputs:
- output 1: float32 [4], P('dp'), parts along dimension 0
- output 2: float32 [64, 128, 512], P(('dp', 'stage')), parts along dimension 0
- output 3: float32 [64, 512, 128], P(('dp', 'stage')), parts along dimension 0
- output 4: float32 [122368, 128], P('dp'), parts along dimension 0
There are 4 independent parts. A program takes and returns all parts, laid end to end along the dimension named above; an argument that names none is the same for every part.
All inputs are finite; a program needn't handle non-finite values.
Results may differ from a plain program's by a relative error of at most 0.02.
Values are sent between devices in bfloat16 or wider.
A program may use at most 768 MiB of HBM per device.

v0:
```python
import jax
import jax.numpy as jnp
from jax import lax
from jax.sharding import PartitionSpec as P


def rms_normalize(x_act):
    x_wide = x_act.astype(jnp.float32)
    inv_rms = lax.rsqrt(jnp.mean(x_wide * x_wide, axis=-1, keepdims=True) + 1e-6)
    return (x_wide * inv_rms).astype(jnp.bfloat16)


def block_forward(x_act, w_up, w_down):
    pre_act = jnp.dot(x_act, w_up, preferred_element_type=jnp.float32).astype(jnp.bfloat16)
    hidden = jax.nn.gelu(pre_act.astype(jnp.float32)).astype(jnp.bfloat16)
    branch = jnp.dot(hidden, w_down, preferred_element_type=jnp.float32)
    return (x_act.astype(jnp.float32) + branch).astype(jnp.bfloat16), pre_act, hidden


def block_backward(x_act, pre_act, hidden, grad_out, w_up, w_down):
    grad_down = jnp.einsum("tf,td->fd", hidden, grad_out, preferred_element_type=jnp.float32)
    grad_hidden = jnp.einsum("td,fd->tf", grad_out, w_down, preferred_element_type=jnp.float32).astype(jnp.bfloat16)
    gelu_vjp = jax.vjp(jax.nn.gelu, pre_act.astype(jnp.float32))[1]
    grad_pre = gelu_vjp(grad_hidden.astype(jnp.float32))[0].astype(jnp.bfloat16)
    grad_up = jnp.einsum("td,tf->df", x_act, grad_pre, preferred_element_type=jnp.float32)
    back_flow = jnp.einsum("tf,df->td", grad_pre, w_up, preferred_element_type=jnp.float32)
    grad_in = (grad_out.astype(jnp.float32) + back_flow).astype(jnp.bfloat16)
    return grad_in, grad_up, grad_down


def head_step(x_act, lab_row, emb_table, grad_emb, inv_count):
    logit_scale = emb_table.shape[1] ** -0.5
    normed, norm_vjp = jax.vjp(rms_normalize, x_act)
    logits = (jnp.einsum("td,vd->tv", normed, emb_table, preferred_element_type=jnp.float32) * logit_scale).astype(jnp.bfloat16)
    logit_f = logits.astype(jnp.float32)
    row_max = jnp.max(logit_f, axis=-1, keepdims=True)
    exp_shift = jnp.exp(logit_f - row_max)
    exp_total = jnp.sum(exp_shift, axis=-1, keepdims=True)
    is_label = lax.broadcasted_iota(jnp.int32, logit_f.shape, 1) == lab_row[:, None]
    picked = jnp.sum(jnp.where(is_label, logit_f, 0.0), axis=-1)
    loss_part = jnp.sum(row_max[:, 0] + jnp.log(exp_total[:, 0]) - picked) * inv_count
    grad_logits = ((exp_shift / exp_total - is_label.astype(jnp.float32)) * inv_count).astype(jnp.bfloat16)
    grad_emb = grad_emb + jnp.einsum("tv,td->vd", grad_logits, normed, preferred_element_type=jnp.float32) * logit_scale
    grad_normed = (jnp.einsum("tv,vd->td", grad_logits, emb_table, preferred_element_type=jnp.float32) * logit_scale).astype(jnp.bfloat16)
    return norm_vjp(grad_normed)[0], grad_emb, loss_part


def solution(mesh):
    n_stage = mesh.shape["stage"]
    fwd_perm = [(stage_id, stage_id + 1) for stage_id in range(n_stage - 1)]
    bwd_perm = [(stage_id + 1, stage_id) for stage_id in range(n_stage - 1)]

    def device_fn(tokens, labels, emb_table, w_up, w_down):
        n_micro, seq_len = tokens.shape
        vocab_rows, model_dim = emb_table.shape
        w_up = w_up[0]
        w_down = w_down[0]
        ffn_dim = w_up.shape[1]
        stage_idx = lax.axis_index("stage")
        is_first = stage_idx == 0
        is_last = stage_idx == n_stage - 1
        n_slots = min(n_micro, 2 * n_stage - 1)
        n_ticks = n_micro + 2 * n_stage - 2
        inv_count = 1.0 / (n_micro * seq_len)

        def tick(tick_idx, loop_state):
            recv_act, recv_grad, stash_x, stash_pre, stash_hid, acc_up, acc_down, grad_emb, loss_acc = loop_state
            micro_f = tick_idx - stage_idx
            fwd_ok = (micro_f >= 0) & (micro_f < n_micro)
            idx_f = jnp.clip(micro_f, 0, n_micro - 1)
            slot_f = idx_f % n_slots
            micro_b = tick_idx - (2 * n_stage - 2) + stage_idx
            bwd_ok = (micro_b >= 0) & (micro_b < n_micro)
            idx_b = jnp.clip(micro_b, 0, n_micro - 1)
            slot_b = idx_b % n_slots
            tok_f = lax.dynamic_index_in_dim(tokens, idx_f, 0, keepdims=False)
            lab_f = lax.dynamic_index_in_dim(labels, idx_f, 0, keepdims=False)
            x_in = jnp.where(is_first, jnp.take(emb_table, tok_f, axis=0), recv_act)

            def run_fwd(branch_in):
                y_out, pre_act, hidden = block_forward(x_in, w_up, w_down)
                return (y_out, lax.dynamic_update_index_in_dim(branch_in[0], x_in, slot_f, 0), lax.dynamic_update_index_in_dim(branch_in[1], pre_act, slot_f, 0), lax.dynamic_update_index_in_dim(branch_in[2], hidden, slot_f, 0))

            def skip_fwd(branch_in):
                return (jnp.zeros_like(x_in),) + branch_in

            y_out, stash_x, stash_pre, stash_hid = lax.cond(fwd_ok, run_fwd, skip_fwd, (stash_x, stash_pre, stash_hid))

            def run_head(branch_in):
                grad_x, new_emb, loss_part = head_step(y_out, lab_f, emb_table, branch_in[0], inv_count)
                return grad_x, new_emb, branch_in[1] + loss_part

            def skip_head(branch_in):
                return jnp.zeros_like(y_out), branch_in[0], branch_in[1]

            head_grad, grad_emb, loss_acc = lax.cond(is_last & fwd_ok, run_head, skip_head, (grad_emb, loss_acc))
            grad_out = jnp.where(is_last, head_grad, recv_grad)

            def run_bwd(branch_in):
                x_saved = lax.dynamic_index_in_dim(stash_x, slot_b, 0, keepdims=False)
                pre_saved = lax.dynamic_index_in_dim(stash_pre, slot_b, 0, keepdims=False)
                hid_saved = lax.dynamic_index_in_dim(stash_hid, slot_b, 0, keepdims=False)
                grad_in, g_up, g_down = block_backward(x_saved, pre_saved, hid_saved, grad_out, w_up, w_down)
                return grad_in, branch_in[0] + g_up, branch_in[1] + g_down

            def skip_bwd(branch_in):
                return jnp.zeros_like(grad_out), branch_in[0], branch_in[1]

            grad_in, acc_up, acc_down = lax.cond(bwd_ok, run_bwd, skip_bwd, (acc_up, acc_down))
            tok_b = lax.dynamic_index_in_dim(tokens, idx_b, 0, keepdims=False)
            emb_rows = jnp.where(is_first, grad_in, jnp.zeros_like(grad_in)).astype(jnp.float32)
            grad_emb = grad_emb.at[tok_b].add(emb_rows)
            recv_act = lax.ppermute(y_out, "stage", fwd_perm)
            recv_grad = lax.ppermute(grad_in, "stage", bwd_perm)
            return (recv_act, recv_grad, stash_x, stash_pre, stash_hid, acc_up, acc_down, grad_emb, loss_acc)

        zeros_act = jnp.zeros((seq_len, model_dim), jnp.bfloat16)
        init_carry = (zeros_act, zeros_act, jnp.zeros((n_slots, seq_len, model_dim), jnp.bfloat16), jnp.zeros((n_slots, seq_len, ffn_dim), jnp.bfloat16), jnp.zeros((n_slots, seq_len, ffn_dim), jnp.bfloat16), jnp.zeros((model_dim, ffn_dim), jnp.float32), jnp.zeros((ffn_dim, model_dim), jnp.float32), jnp.zeros((vocab_rows, model_dim), jnp.float32), jnp.zeros((), jnp.float32))
        final_state = lax.fori_loop(0, n_ticks, tick, init_carry)
        grad_emb = lax.psum(final_state[7], "stage")
        loss_total = lax.psum(final_state[8], "stage")
        return loss_total.reshape(1), final_state[5][None], final_state[6][None], grad_emb

    return jax.shard_map(device_fn, mesh=mesh, in_specs=(P("dp", None), P("dp", None), P(None, None), P("stage", None, None), P("stage", None, None)), out_specs=(P("dp"), P(("dp", "stage"), None, None), P(("dp", "stage"), None, None), P("dp", None)), check_vma=False)
```

profile of v0, /device:TPU:21, one launch (start us, length us, event | category | flops | bytes accessed | tf_op | source)
XLA Modules:
  0.0 1760.8 jit_solution(3433800912084277095)
XLA Ops:
  13.6 1539.4 %while.31 = (s32[]{:T(128)}, bf16[64,128]{1,0:T(8,128)(2,1)S(1)}, bf16[64,128]{1,0:T(8,128)(2,1)S(1)}, bf16[16,64,128]{2,1,0:T(8,128)(2,1)S(1)}, bf16[16,64,512]...) while((s32[]{:T(128)}, bf16[64,128]{1,0:T(8,128)(2,1)S(1)}, ...), condition=%wide.region_14.15_spmd, body=%wide.region_0.14_spmd.sunk | while | flops 1612613888 | bytes 96764288 | solution.py:119
  131.6 12.1 scatter_custom_fusion.5
  157.5 12.1 scatter_custom_fusion.5
  183.4 12.1 scatter_custom_fusion.5
  209.3 12.1 scatter_custom_fusion.5
  235.2 12.1 scatter_custom_fusion.5
  364.7 12.1 scatter_custom_fusion.5
  390.6 12.1 scatter_custom_fusion.5
  416.5 12.1 scatter_custom_fusion.5
  442.4 12.1 scatter_custom_fusion.5
  468.3 12.1 scatter_custom_fusion.5
  510.5 12.1 scatter_custom_fusion.5
  554.1 12.1 scatter_custom_fusion.5
  574.5 12.1 scatter_custom_fusion.5
  622.0 12.1 scatter_custom_fusion.5
  641.4 27.6 %collective-permute-start = (bf16[64,128]{1,0:T(8,128)(2,1)}, bf16[64,128]{1,0:T(8,128)(2,1)S(1)}, u32[]{:S(2)}, u32[]{:S(2)}) collective-permute-start(bf16[64,128]{1,0:T(8,128)(2,1)} %get-tuple-element.1044), channel_id=1, source_target_pairs={{0,1},{1,2},{2,3},{3,4},{4,5},{5,6},{6,7},{7,8},{8,9},{9,10},{10,1... | collective-permute-start | bytes 49160 | tf_op jit(solution)/shard_map/while/body/eval_jaxpr/ppermute | solution.py:113
  671.8 12.1 scatter_custom_fusion.5
  690.6 34.3 %collective-permute-start = (bf16[64,128]{1,0:T(8,128)(2,1)}, bf16[64,128]{1,0:T(8,128)(2,1)S(1)}, u32[]{:S(2)}, u32[]{:S(2)}) collective-permute-start(bf16[64,128]{1,0:T(8,128)(2,1)} %get-tuple-element.1044), channel_id=1, source_target_pairs={{0,1},{1,2},{2,3},{3,4},{4,5},{5,6},{6,7},{7,8},{8,9},{9,10},{10,1... | collective-permute-start | bytes 49160 | tf_op jit(solution)/shard_map/while/body/eval_jaxpr/ppermute | solution.py:113
  746.5 27.6 %collective-permute-start = (bf16[64,128]{1,0:T(8,128)(2,1)}, bf16[64,128]{1,0:T(8,128)(2,1)S(1)}, u32[]{:S(2)}, u32[]{:S(2)}) collective-permute-start(bf16[64,128]{1,0:T(8,128)(2,1)} %get-tuple-element.1044), channel_id=1, source_target_pairs={{0,1},{1,2},{2,3},{3,4},{4,5},{5,6},{6,7},{7,8},{8,9},{9,10},{10,1... | collective-permute-start | bytes 49160 | tf_op jit(solution)/shard_map/while/body/eval_jaxpr/ppermute | solution.py:113
  776.8 12.1 scatter_custom_fusion.5
  788.9 12.8 collective-permute-done.1
  802.4 27.6 %collective-permute-start = (bf16[64,128]{1,0:T(8,128)(2,1)}, bf16[64,128]{1,0:T(8,128)(2,1)S(1)}, u32[]{:S(2)}, u32[]{:S(2)}) collective-permute-start(bf16[64,128]{1,0:T(8,128)(2,1)} %get-tuple-element.1044), channel_id=1, source_target_pairs={{0,1},{1,2},{2,3},{3,4},{4,5},{5,6},{6,7},{7,8},{8,9},{9,10},{10,1... | collective-permute-start | bytes 49160 | tf_op jit(solution)/shard_map/while/body/eval_jaxpr/ppermute | solution.py:113
  832.7 12.1 scatter_custom_fusion.5
  851.5 33.4 %collective-permute-start = (bf16[64,128]{1,0:T(8,128)(2,1)}, bf16[64,128]{1,0:T(8,128)(2,1)S(1)}, u32[]{:S(2)}, u32[]{:S(2)}) collective-permute-start(bf16[64,128]{1,0:T(8,128)(2,1)} %get-tuple-element.1044), channel_id=1, source_target_pairs={{0,1},{1,2},{2,3},{3,4},{4,5},{5,6},{6,7},{7,8},{8,9},{9,10},{10,1... | collective-permute-start | bytes 49160 | tf_op jit(solution)/shard_map/while/body/eval_jaxpr/ppermute | solution.py:113
  906.5 26.7 %collective-permute-start = (bf16[64,128]{1,0:T(8,128)(2,1)}, bf16[64,128]{1,0:T(8,128)(2,1)S(1)}, u32[]{:S(2)}, u32[]{:S(2)}) collective-permute-start(bf16[64,128]{1,0:T(8,128)(2,1)} %get-tuple-element.1044), channel_id=1, source_target_pairs={{0,1},{1,2},{2,3},{3,4},{4,5},{5,6},{6,7},{7,8},{8,9},{9,10},{10,1... | collective-permute-start | bytes 49160 | tf_op jit(solution)/shard_map/while/body/eval_jaxpr/ppermute | solution.py:113
  961.6 26.7 %collective-permute-start = (bf16[64,128]{1,0:T(8,128)(2,1)}, bf16[64,128]{1,0:T(8,128)(2,1)S(1)}, u32[]{:S(2)}, u32[]{:S(2)}) collective-permute-start(bf16[64,128]{1,0:T(8,128)(2,1)} %get-tuple-element.1044), channel_id=1, source_target_pairs={{0,1},{1,2},{2,3},{3,4},{4,5},{5,6},{6,7},{7,8},{8,9},{9,10},{10,1... | collective-permute-start | bytes 49160 | tf_op jit(solution)/shard_map/while/body/eval_jaxpr/ppermute | solution.py:113
  1009.9 33.4 %collective-permute-start = (bf16[64,128]{1,0:T(8,128)(2,1)}, bf16[64,128]{1,0:T(8,128)(2,1)S(1)}, u32[]{:S(2)}, u32[]{:S(2)}) collective-permute-start(bf16[64,128]{1,0:T(8,128)(2,1)} %get-tuple-element.1044), channel_id=1, source_target_pairs={{0,1},{1,2},{2,3},{3,4},{4,5},{5,6},{6,7},{7,8},{8,9},{9,10},{10,1... | collective-permute-start | bytes 49160 | tf_op jit(solution)/shard_map/while/body/eval_jaxpr/ppermute | solution.py:113
  1064.9 26.7 %collective-permute-start = (bf16[64,128]{1,0:T(8,128)(2,1)}, bf16[64,128]{1,0:T(8,128)(2,1)S(1)}, u32[]{:S(2)}, u32[]{:S(2)}) collective-permute-start(bf16[64,128]{1,0:T(8,128)(2,1)} %get-tuple-element.1044), channel_id=1, source_target_pairs={{0,1},{1,2},{2,3},{3,4},{4,5},{5,6},{6,7},{7,8},{8,9},{9,10},{10,1... | collective-permute-start | bytes 49160 | tf_op jit(solution)/shard_map/while/body/eval_jaxpr/ppermute | solution.py:113
  1119.9 26.7 %collective-permute-start = (bf16[64,128]{1,0:T(8,128)(2,1)}, bf16[64,128]{1,0:T(8,128)(2,1)S(1)}, u32[]{:S(2)}, u32[]{:S(2)}) collective-permute-start(bf16[64,128]{1,0:T(8,128)(2,1)} %get-tuple-element.1044), channel_id=1, source_target_pairs={{0,1},{1,2},{2,3},{3,4},{4,5},{5,6},{6,7},{7,8},{8,9},{9,10},{10,1... | collective-permute-start | bytes 49160 | tf_op jit(solution)/shard_map/while/body/eval_jaxpr/ppermute | solution.py:113
  1150.3 12.1 scatter_custom_fusion.5
  1168.2 33.4 %collective-permute-start = (bf16[64,128]{1,0:T(8,128)(2,1)}, bf16[64,128]{1,0:T(8,128)(2,1)S(1)}, u32[]{:S(2)}, u32[]{:S(2)}) collective-permute-start(bf16[64,128]{1,0:T(8,128)(2,1)} %get-tuple-element.1044), channel_id=1, source_target_pairs={{0,1},{1,2},{2,3},{3,4},{4,5},{5,6},{6,7},{7,8},{8,9},{9,10},{10,1... | collective-permute-start | bytes 49160 | tf_op jit(solution)/shard_map/while/body/eval_jaxpr/ppermute | solution.py:113
  1205.3 12.1 scatter_custom_fusion.5
  1223.3 26.7 %collective-permute-start = (bf16[64,128]{1,0:T(8,128)(2,1)}, bf16[64,128]{1,0:T(8,128)(2,1)S(1)}, u32[]{:S(2)}, u32[]{:S(2)}) collective-permute-start(bf16[64,128]{1,0:T(8,128)(2,1)} %get-tuple-element.1044), channel_id=1, source_target_pairs={{0,1},{1,2},{2,3},{3,4},{4,5},{5,6},{6,7},{7,8},{8,9},{9,10},{10,1... | collective-permute-start | bytes 49160 | tf_op jit(solution)/shard_map/while/body/eval_jaxpr/ppermute | solution.py:113
  1253.6 12.1 scatter_custom_fusion.5
  1278.3 26.7 %collective-permute-start = (bf16[64,128]{1,0:T(8,128)(2,1)}, bf16[64,128]{1,0:T(8,128)(2,1)S(1)}, u32[]{:S(2)}, u32[]{:S(2)}) collective-permute-start(bf16[64,128]{1,0:T(8,128)(2,1)} %get-tuple-element.1044), channel_id=1, source_target_pairs={{0,1},{1,2},{2,3},{3,4},{4,5},{5,6},{6,7},{7,8},{8,9},{9,10},{10,1... | collective-permute-start | bytes 49160 | tf_op jit(solution)/shard_map/while/body/eval_jaxpr/ppermute | solution.py:113
  1308.7 12.1 scatter_custom_fusion.5
  1326.6 13.3 collective-permute-start
  1343.6 12.1 scatter_custom_fusion.5
  1356.3 13.3 collective-permute-start
  1386.0 13.3 collective-permute-start
  1415.7 13.3 collective-permute-start
  1432.6 12.1 scatter_custom_fusion.5
  1445.4 13.3 collective-permute-start
  1475.1 13.3 collective-permute-start
  1492.0 12.1 scatter_custom_fusion.5
  1504.8 13.3 collective-permute-start
  1553.8 28.6 %psum.14 = f32[1]{0:T(128)} all-reduce(f32[1]{0:T(128)} %bitcast.15), channel_id=1, replica_groups=mesh['dp'=4,'stage'=16] {'stage'}, use_global_device_ids=true, to_apply=%region_15.16 | all-reduce | flops 1 | bytes 8 | tf_op jit(solution)/shard_map/psum | solution.py:121
  1582.4 160.7 %all-reduce.2.cloned.1.call-done = f32[30592,128]{1,0:T(8,128)} async-done(((f32[30592,128]{1,0:T(8,128)}), f32[30592,128]{1,0:T(8,128)}) %all-reduce.2.cloned.1.call-update) | async-done | bytes 15663120 | tf_op jit(solution)/shard_map/psum | solution.py:120
  (824 shorter events, 929.2 us)
Async XLA Ops:
  7.2 1735.9 %all-reduce.2.cloned.1.call-start = ((), (), s32[]{:S(2)}) async-start(), calls=%async_computation | async-start | bytes 31326208 | tf_op jit(solution)/shard_map/psum | solution.py:120
  14.3 27.5 %collective-permute-start = (bf16[64,128]{1,0:T(8,128)(2,1)}, bf16[64,128]{1,0:T(8,128)(2,1)S(1)}, u32[]{:S(2)}, u32[]{:S(2)}) collective-permute-start(bf16[64,128]{1,0:T(8,128)(2,1)} %get-tuple-element.1044), channel_id=1, source_target_pairs={{0,1},{1,2},{2,3},{3,4},{4,5},{5,6},{6,7},{7,8},{8,9},{9,10},{10,1... | collective-permute-start | bytes 49160 | tf_op jit(solution)/shard_map/while/body/eval_jaxpr/ppermute | solution.py:113
  19.5 22.3 %collective-permute-start.1 = (bf16[64,128]{1,0:T(8,128)(2,1)S(1)}, bf16[64,128]{1,0:T(8,128)(2,1)S(1)}, u32[]{:S(2)}, u32[]{:S(2)}) collective-permute-start(bf16[64,128]{1,0:T(8,128)(2,1)S(1)} %get-tuple-element.1049), channel_id=1, source_target_pairs={{1,0},{2,1},{3,2},{4,3},{5,4},{6,5},{7,6},{8,7},{9,8},{10,9},{11,1... | collective-permute-start | bytes 49160 | tf_op jit(solution)/shard_map/while/body/eval_jaxpr/ppermute | solution.py:114
  99.2 18.5 %collective-permute-start = (bf16[64,128]{1,0:T(8,128)(2,1)}, bf16[64,128]{1,0:T(8,128)(2,1)S(1)}, u32[]{:S(2)}, u32[]{:S(2)}) collective-permute-start(bf16[64,128]{1,0:T(8,128)(2,1)} %get-tuple-element.1044), channel_id=1, source_target_pairs={{0,1},{1,2},{2,3},{3,4},{4,5},{5,6},{6,7},{7,8},{8,9},{9,10},{10,1... | collective-permute-start | bytes 49160 | tf_op jit(solution)/shard_map/while/body/eval_jaxpr/ppermute | solution.py:113
  125.2 18.5 %collective-permute-start = (bf16[64,128]{1,0:T(8,128)(2,1)}, bf16[64,128]{1,0:T(8,128)(2,1)S(1)}, u32[]{:S(2)}, u32[]{:S(2)}) collective-permute-start(bf16[64,128]{1,0:T(8,128)(2,1)} %get-tuple-element.1044), channel_id=1, source_target_pairs={{0,1},{1,2},{2,3},{3,4},{4,5},{5,6},{6,7},{7,8},{8,9},{9,10},{10,1... | collective-permute-start | bytes 49160 | tf_op jit(solution)/shard_map/while/body/eval_jaxpr/ppermute | solution.py:113
  455.2 25.2 %collective-permute-start = (bf16[64,128]{1,0:T(8,128)(2,1)}, bf16[64,128]{1,0:T(8,128)(2,1)S(1)}, u32[]{:S(2)}, u32[]{:S(2)}) collective-permute-start(bf16[64,128]{1,0:T(8,128)(2,1)} %get-tuple-element.1044), channel_id=1, source_target_pairs={{0,1},{1,2},{2,3},{3,4},{4,5},{5,6},{6,7},{7,8},{8,9},{9,10},{10,1... | collective-permute-start | bytes 49160 | tf_op jit(solution)/shard_map/while/body/eval_jaxpr/ppermute | solution.py:113
  481.1 18.5 %collective-permute-start = (bf16[64,128]{1,0:T(8,128)(2,1)}, bf16[64,128]{1,0:T(8,128)(2,1)S(1)}, u32[]{:S(2)}, u32[]{:S(2)}) collective-permute-start(bf16[64,128]{1,0:T(8,128)(2,1)} %get-tuple-element.1044), channel_id=1, source_target_pairs={{0,1},{1,2},{2,3},{3,4},{4,5},{5,6},{6,7},{7,8},{8,9},{9,10},{10,1... | collective-permute-start | bytes 49160 | tf_op jit(solution)/shard_map/while/body/eval_jaxpr/ppermute | solution.py:113
  500.3 22.3 %collective-permute-start = (bf16[64,128]{1,0:T(8,128)(2,1)}, bf16[64,128]{1,0:T(8,128)(2,1)S(1)}, u32[]{:S(2)}, u32[]{:S(2)}) collective-permute-start(bf16[64,128]{1,0:T(8,128)(2,1)} %get-tuple-element.1044), channel_id=1, source_target_pairs={{0,1},{1,2},{2,3},{3,4},{4,5},{5,6},{6,7},{7,8},{8,9},{9,10},{10,1... | collective-permute-start | bytes 49160 | tf_op jit(solution)/shard_map/while/body/eval_jaxpr/ppermute | solution.py:113
  523.2 18.5 %collective-permute-start = (bf16[64,128]{1,0:T(8,128)(2,1)}, bf16[64,128]{1,0:T(8,128)(2,1)S(1)}, u32[]{:S(2)}, u32[]{:S(2)}) collective-permute-start(bf16[64,128]{1,0:T(8,128)(2,1)} %get-tuple-element.1044), channel_id=1, source_target_pairs={{0,1},{1,2},{2,3},{3,4},{4,5},{5,6},{6,7},{7,8},{8,9},{9,10},{10,1... | collective-permute-start | bytes 49160 | tf_op jit(solution)/shard_map/while/body/eval_jaxpr/ppermute | solution.py:113
  542.4 23.8 %collective-permute-start = (bf16[64,128]{1,0:T(8,128)(2,1)}, bf16[64,128]{1,0:T(8,128)(2,1)S(1)}, u32[]{:S(2)}, u32[]{:S(2)}) collective-permute-start(bf16[64,128]{1,0:T(8,128)(2,1)} %get-tuple-element.1044), channel_id=1, source_target_pairs={{0,1},{1,2},{2,3},{3,4},{4,5},{5,6},{6,7},{7,8},{8,9},{9,10},{10,1... | collective-permute-start | bytes 49160 | tf_op jit(solution)/shard_map/while/body/eval_jaxpr/ppermute | solution.py:113
  566.9 19.7 %collective-permute-start = (bf16[64,128]{1,0:T(8,128)(2,1)}, bf16[64,128]{1,0:T(8,128)(2,1)S(1)}, u32[]{:S(2)}, u32[]{:S(2)}) collective-permute-start(bf16[64,128]{1,0:T(8,128)(2,1)} %get-tuple-element.1044), channel_id=1, source_target_pairs={{0,1},{1,2},{2,3},{3,4},{4,5},{5,6},{6,7},{7,8},{8,9},{9,10},{10,1... | collective-permute-start | bytes 49160 | tf_op jit(solution)/shard_map/while/body/eval_jaxpr/ppermute | solution.py:113
  587.3 26.5 %collective-permute-start = (bf16[64,128]{1,0:T(8,128)(2,1)}, bf16[64,128]{1,0:T(8,128)(2,1)S(1)}, u32[]{:S(2)}, u32[]{:S(2)}) collective-permute-start(bf16[64,128]{1,0:T(8,128)(2,1)} %get-tuple-element.1044), channel_id=1, source_target_pairs={{0,1},{1,2},{2,3},{3,4},{4,5},{5,6},{6,7},{7,8},{8,9},{9,10},{10,1... | collective-permute-start | bytes 49160 | tf_op jit(solution)/shard_map/while/body/eval_jaxpr/ppermute | solution.py:113
  614.4 26.4 %collective-permute-start = (bf16[64,128]{1,0:T(8,128)(2,1)}, bf16[64,128]{1,0:T(8,128)(2,1)S(1)}, u32[]{:S(2)}, u32[]{:S(2)}) collective-permute-start(bf16[64,128]{1,0:T(8,128)(2,1)} %get-tuple-element.1044), channel_id=1, source_target_pairs={{0,1},{1,2},{2,3},{3,4},{4,5},{5,6},{6,7},{7,8},{8,9},{9,10},{10,1... | collective-permute-start | bytes 49160 | tf_op jit(solution)/shard_map/while/body/eval_jaxpr/ppermute | solution.py:113
  619.4 21.4 %collective-permute-start.1 = (bf16[64,128]{1,0:T(8,128)(2,1)S(1)}, bf16[64,128]{1,0:T(8,128)(2,1)S(1)}, u32[]{:S(2)}, u32[]{:S(2)}) collective-permute-start(bf16[64,128]{1,0:T(8,128)(2,1)S(1)} %get-tuple-element.1049), channel_id=1, source_target_pairs={{1,0},{2,1},{3,2},{4,3},{5,4},{6,5},{7,6},{8,7},{9,8},{10,9},{11,1... | collective-permute-start | bytes 49160 | tf_op jit(solution)/shard_map/while/body/eval_jaxpr/ppermute | solution.py:114
  641.4 48.5 %collective-permute-start = (bf16[64,128]{1,0:T(8,128)(2,1)}, bf16[64,128]{1,0:T(8,128)(2,1)S(1)}, u32[]{:S(2)}, u32[]{:S(2)}) collective-permute-start(bf16[64,128]{1,0:T(8,128)(2,1)} %get-tuple-element.1044), channel_id=1, source_target_pairs={{0,1},{1,2},{2,3},{3,4},{4,5},{5,6},{6,7},{7,8},{8,9},{9,10},{10,1... | collective-permute-start | bytes 49160 | tf_op jit(solution)/shard_map/while/body/eval_jaxpr/ppermute | solution.py:113
  669.1 20.8 %collective-permute-start.1 = (bf16[64,128]{1,0:T(8,128)(2,1)S(1)}, bf16[64,128]{1,0:T(8,128)(2,1)S(1)}, u32[]{:S(2)}, u32[]{:S(2)}) collective-permute-start(bf16[64,128]{1,0:T(8,128)(2,1)S(1)} %get-tuple-element.1049), channel_id=1, source_target_pairs={{1,0},{2,1},{3,2},{4,3},{5,4},{6,5},{7,6},{8,7},{9,8},{10,9},{11,1... | collective-permute-start | bytes 49160 | tf_op jit(solution)/shard_map/while/body/eval_jaxpr/ppermute | solution.py:114
  690.6 55.2 %collective-permute-start = (bf16[64,128]{1,0:T(8,128)(2,1)}, bf16[64,128]{1,0:T(8,128)(2,1)S(1)}, u32[]{:S(2)}, u32[]{:S(2)}) collective-permute-start(bf16[64,128]{1,0:T(8,128)(2,1)} %get-tuple-element.1044), channel_id=1, source_target_pairs={{0,1},{1,2},{2,3},{3,4},{4,5},{5,6},{6,7},{7,8},{8,9},{9,10},{10,1... | collective-permute-start | bytes 49160 | tf_op jit(solution)/shard_map/while/body/eval_jaxpr/ppermute | solution.py:113
  725.0 20.8 %collective-permute-start.1 = (bf16[64,128]{1,0:T(8,128)(2,1)S(1)}, bf16[64,128]{1,0:T(8,128)(2,1)S(1)}, u32[]{:S(2)}, u32[]{:S(2)}) collective-permute-start(bf16[64,128]{1,0:T(8,128)(2,1)S(1)} %get-tuple-element.1049), channel_id=1, source_target_pairs={{1,0},{2,1},{3,2},{4,3},{5,4},{6,5},{7,6},{8,7},{9,8},{10,9},{11,1... | collective-permute-start | bytes 49160 | tf_op jit(solution)/shard_map/while/body/eval_jaxpr/ppermute | solution.py:114
  746.5 55.2 %collective-permute-start = (bf16[64,128]{1,0:T(8,128)(2,1)}, bf16[64,128]{1,0:T(8,128)(2,1)S(1)}, u32[]{:S(2)}, u32[]{:S(2)}) collective-permute-start(bf16[64,128]{1,0:T(8,128)(2,1)} %get-tuple-element.1044), channel_id=1, source_target_pairs={{0,1},{1,2},{2,3},{3,4},{4,5},{5,6},{6,7},{7,8},{8,9},{9,10},{10,1... | collective-permute-start | bytes 49160 | tf_op jit(solution)/shard_map/while/body/eval_jaxpr/ppermute | solution.py:113
  774.2 27.5 %collective-permute-start.1 = (bf16[64,128]{1,0:T(8,128)(2,1)S(1)}, bf16[64,128]{1,0:T(8,128)(2,1)S(1)}, u32[]{:S(2)}, u32[]{:S(2)}) collective-permute-start(bf16[64,128]{1,0:T(8,128)(2,1)S(1)} %get-tuple-element.1049), channel_id=1, source_target_pairs={{1,0},{2,1},{3,2},{4,3},{5,4},{6,5},{7,6},{8,7},{9,8},{10,9},{11,1... | collective-permute-start | bytes 49160 | tf_op jit(solution)/shard_map/while/body/eval_jaxpr/ppermute | solution.py:114
  802.4 48.5 %collective-permute-start = (bf16[64,128]{1,0:T(8,128)(2,1)}, bf16[64,128]{1,0:T(8,128)(2,1)S(1)}, u32[]{:S(2)}, u32[]{:S(2)}) collective-permute-start(bf16[64,128]{1,0:T(8,128)(2,1)} %get-tuple-element.1044), channel_id=1, source_target_pairs={{0,1},{1,2},{2,3},{3,4},{4,5},{5,6},{6,7},{7,8},{8,9},{9,10},{10,1... | collective-permute-start | bytes 49160 | tf_op jit(solution)/shard_map/while/body/eval_jaxpr/ppermute | solution.py:113
  830.1 20.8 %collective-permute-start.1 = (bf16[64,128]{1,0:T(8,128)(2,1)S(1)}, bf16[64,128]{1,0:T(8,128)(2,1)S(1)}, u32[]{:S(2)}, u32[]{:S(2)}) collective-permute-start(bf16[64,128]{1,0:T(8,128)(2,1)S(1)} %get-tuple-element.1049), channel_id=1, source_target_pairs={{1,0},{2,1},{3,2},{4,3},{5,4},{6,5},{7,6},{8,7},{9,8},{10,9},{11,1... | collective-permute-start | bytes 49160 | tf_op jit(solution)/shard_map/while/body/eval_jaxpr/ppermute | solution.py:114
  851.5 54.4 %collective-permute-start = (bf16[64,128]{1,0:T(8,128)(2,1)}, bf16[64,128]{1,0:T(8,128)(2,1)S(1)}, u32[]{:S(2)}, u32[]{:S(2)}) collective-permute-start(bf16[64,128]{1,0:T(8,128)(2,1)} %get-tuple-element.1044), channel_id=1, source_target_pairs={{0,1},{1,2},{2,3},{3,4},{4,5},{5,6},{6,7},{7,8},{8,9},{9,10},{10,1... | collective-permute-start | bytes 49160 | tf_op jit(solution)/shard_map/while/body/eval_jaxpr/ppermute | solution.py:113
  885.9 20.0 %collective-permute-start.1 = (bf16[64,128]{1,0:T(8,128)(2,1)S(1)}, bf16[64,128]{1,0:T(8,128)(2,1)S(1)}, u32[]{:S(2)}, u32[]{:S(2)}) collective-permute-start(bf16[64,128]{1,0:T(8,128)(2,1)S(1)} %get-tuple-element.1049), channel_id=1, source_target_pairs={{1,0},{2,1},{3,2},{4,3},{5,4},{6,5},{7,6},{8,7},{9,8},{10,9},{11,1... | collective-permute-start | bytes 49160 | tf_op jit(solution)/shard_map/while/body/eval_jaxpr/ppermute | solution.py:114
  906.5 54.4 %collective-permute-start = (bf16[64,128]{1,0:T(8,128)(2,1)}, bf16[64,128]{1,0:T(8,128)(2,1)S(1)}, u32[]{:S(2)}, u32[]{:S(2)}) collective-permute-start(bf16[64,128]{1,0:T(8,128)(2,1)} %get-tuple-element.1044), channel_id=1, source_target_pairs={{0,1},{1,2},{2,3},{3,4},{4,5},{5,6},{6,7},{7,8},{8,9},{9,10},{10,1... | collective-permute-start | bytes 49160 | tf_op jit(solution)/shard_map/while/body/eval_jaxpr/ppermute | solution.py:113
  934.2 26.7 %collective-permute-start.1 = (bf16[64,128]{1,0:T(8,128)(2,1)S(1)}, bf16[64,128]{1,0:T(8,128)(2,1)S(1)}, u32[]{:S(2)}, u32[]{:S(2)}) collective-permute-start(bf16[64,128]{1,0:T(8,128)(2,1)S(1)} %get-tuple-element.1049), channel_id=1, source_target_pairs={{1,0},{2,1},{3,2},{4,3},{5,4},{6,5},{7,6},{8,7},{9,8},{10,9},{11,1... | collective-permute-start | bytes 49160 | tf_op jit(solution)/shard_map/while/body/eval_jaxpr/ppermute | solution.py:114
  961.6 47.7 %collective-permute-start = (bf16[64,128]{1,0:T(8,128)(2,1)}, bf16[64,128]{1,0:T(8,128)(2,1)S(1)}, u32[]{:S(2)}, u32[]{:S(2)}) collective-permute-start(bf16[64,128]{1,0:T(8,128)(2,1)} %get-tuple-element.1044), channel_id=1, source_target_pairs={{0,1},{1,2},{2,3},{3,4},{4,5},{5,6},{6,7},{7,8},{8,9},{9,10},{10,1... | collective-permute-start | bytes 49160 | tf_op jit(solution)/shard_map/while/body/eval_jaxpr/ppermute | solution.py:113
  989.3 20.0 %collective-permute-start.1 = (bf16[64,128]{1,0:T(8,128)(2,1)S(1)}, bf16[64,128]{1,0:T(8,128)(2,1)S(1)}, u32[]{:S(2)}, u32[]{:S(2)}) collective-permute-start(bf16[64,128]{1,0:T(8,128)(2,1)S(1)} %get-tuple-element.1049), channel_id=1, source_target_pairs={{1,0},{2,1},{3,2},{4,3},{5,4},{6,5},{7,6},{8,7},{9,8},{10,9},{11,1... | collective-permute-start | bytes 49160 | tf_op jit(solution)/shard_map/while/body/eval_jaxpr/ppermute | solution.py:114
  1009.9 54.4 %collective-permute-start = (bf16[64,128]{1,0:T(8,128)(2,1)}, bf16[64,128]{1,0:T(8,128)(2,1)S(1)}, u32[]{:S(2)}, u32[]{:S(2)}) collective-permute-start(bf16[64,128]{1,0:T(8,128)(2,1)} %get-tuple-element.1044), channel_id=1, source_target_pairs={{0,1},{1,2},{2,3},{3,4},{4,5},{5,6},{6,7},{7,8},{8,9},{9,10},{10,1... | collective-permute-start | bytes 49160 | tf_op jit(solution)/shard_map/while/body/eval_jaxpr/ppermute | solution.py:113
  1044.3 20.0 %collective-permute-start.1 = (bf16[64,128]{1,0:T(8,128)(2,1)S(1)}, bf16[64,128]{1,0:T(8,128)(2,1)S(1)}, u32[]{:S(2)}, u32[]{:S(2)}) collective-permute-start(bf16[64,128]{1,0:T(8,128)(2,1)S(1)} %get-tuple-element.1049), channel_id=1, source_target_pairs={{1,0},{2,1},{3,2},{4,3},{5,4},{6,5},{7,6},{8,7},{9,8},{10,9},{11,1... | collective-permute-start | bytes 49160 | tf_op jit(solution)/shard_map/while/body/eval_jaxpr/ppermute | solution.py:114
  1064.9 54.4 %collective-permute-start = (bf16[64,128]{1,0:T(8,128)(2,1)}, bf16[64,128]{1,0:T(8,128)(2,1)S(1)}, u32[]{:S(2)}, u32[]{:S(2)}) collective-permute-start(bf16[64,128]{1,0:T(8,128)(2,1)} %get-tuple-element.1044), channel_id=1, source_target_pairs={{0,1},{1,2},{2,3},{3,4},{4,5},{5,6},{6,7},{7,8},{8,9},{9,10},{10,1... | collective-permute-start | bytes 49160 | tf_op jit(solution)/shard_map/while/body/eval_jaxpr/ppermute | solution.py:113
  1092.6 26.7 %collective-permute-start.1 = (bf16[64,128]{1,0:T(8,128)(2,1)S(1)}, bf16[64,128]{1,0:T(8,128)(2,1)S(1)}, u32[]{:S(2)}, u32[]{:S(2)}) collective-permute-start(bf16[64,128]{1,0:T(8,128)(2,1)S(1)} %get-tuple-element.1049), channel_id=1, source_target_pairs={{1,0},{2,1},{3,2},{4,3},{5,4},{6,5},{7,6},{8,7},{9,8},{10,9},{11,1... | collective-permute-start | bytes 49160 | tf_op jit(solution)/shard_map/while/body/eval_jaxpr/ppermute | solution.py:114
  1119.9 47.7 %collective-permute-start = (bf16[64,128]{1,0:T(8,128)(2,1)}, bf16[64,128]{1,0:T(8,128)(2,1)S(1)}, u32[]{:S(2)}, u32[]{:S(2)}) collective-permute-start(bf16[64,128]{1,0:T(8,128)(2,1)} %get-tuple-element.1044), channel_id=1, source_target_pairs={{0,1},{1,2},{2,3},{3,4},{4,5},{5,6},{6,7},{7,8},{8,9},{9,10},{10,1... | collective-permute-start | bytes 49160 | tf_op jit(solution)/shard_map/while/body/eval_jaxpr/ppermute | solution.py:113
  1147.6 20.0 %collective-permute-start.1 = (bf16[64,128]{1,0:T(8,128)(2,1)S(1)}, bf16[64,128]{1,0:T(8,128)(2,1)S(1)}, u32[]{:S(2)}, u32[]{:S(2)}) collective-permute-start(bf16[64,128]{1,0:T(8,128)(2,1)S(1)} %get-tuple-element.1049), channel_id=1, source_target_pairs={{1,0},{2,1},{3,2},{4,3},{5,4},{6,5},{7,6},{8,7},{9,8},{10,9},{11,1... | collective-permute-start | bytes 49160 | tf_op jit(solution)/shard_map/while/body/eval_jaxpr/ppermute | solution.py:114
  1168.2 54.4 %collective-permute-start = (bf16[64,128]{1,0:T(8,128)(2,1)}, bf16[64,128]{1,0:T(8,128)(2,1)S(1)}, u32[]{:S(2)}, u32[]{:S(2)}) collective-permute-start(bf16[64,128]{1,0:T(8,128)(2,1)} %get-tuple-element.1044), channel_id=1, source_target_pairs={{0,1},{1,2},{2,3},{3,4},{4,5},{5,6},{6,7},{7,8},{8,9},{9,10},{10,1... | collective-permute-start | bytes 49160 | tf_op jit(solution)/shard_map/while/body/eval_jaxpr/ppermute | solution.py:113
  1202.7 20.0 %collective-permute-start.1 = (bf16[64,128]{1,0:T(8,128)(2,1)S(1)}, bf16[64,128]{1,0:T(8,128)(2,1)S(1)}, u32[]{:S(2)}, u32[]{:S(2)}) collective-permute-start(bf16[64,128]{1,0:T(8,128)(2,1)S(1)} %get-tuple-element.1049), channel_id=1, source_target_pairs={{1,0},{2,1},{3,2},{4,3},{5,4},{6,5},{7,6},{8,7},{9,8},{10,9},{11,1... | collective-permute-start | bytes 49160 | tf_op jit(solution)/shard_map/while/body/eval_jaxpr/ppermute | solution.py:114
  1223.3 54.4 %collective-permute-start = (bf16[64,128]{1,0:T(8,128)(2,1)}, bf16[64,128]{1,0:T(8,128)(2,1)S(1)}, u32[]{:S(2)}, u32[]{:S(2)}) collective-permute-start(bf16[64,128]{1,0:T(8,128)(2,1)} %get-tuple-element.1044), channel_id=1, source_target_pairs={{0,1},{1,2},{2,3},{3,4},{4,5},{5,6},{6,7},{7,8},{8,9},{9,10},{10,1... | collective-permute-start | bytes 49160 | tf_op jit(solution)/shard_map/while/body/eval_jaxpr/ppermute | solution.py:113
  1251.0 26.7 %collective-permute-start.1 = (bf16[64,128]{1,0:T(8,128)(2,1)S(1)}, bf16[64,128]{1,0:T(8,128)(2,1)S(1)}, u32[]{:S(2)}, u32[]{:S(2)}) collective-permute-start(bf16[64,128]{1,0:T(8,128)(2,1)S(1)} %get-tuple-element.1049), channel_id=1, source_target_pairs={{1,0},{2,1},{3,2},{4,3},{5,4},{6,5},{7,6},{8,7},{9,8},{10,9},{11,1... | collective-permute-start | bytes 49160 | tf_op jit(solution)/shard_map/while/body/eval_jaxpr/ppermute | solution.py:114
  1278.3 47.7 %collective-permute-start = (bf16[64,128]{1,0:T(8,128)(2,1)}, bf16[64,128]{1,0:T(8,128)(2,1)S(1)}, u32[]{:S(2)}, u32[]{:S(2)}) collective-permute-start(bf16[64,128]{1,0:T(8,128)(2,1)} %get-tuple-element.1044), channel_id=1, source_target_pairs={{0,1},{1,2},{2,3},{3,4},{4,5},{5,6},{6,7},{7,8},{8,9},{9,10},{10,1... | collective-permute-start | bytes 49160 | tf_op jit(solution)/shard_map/while/body/eval_jaxpr/ppermute | solution.py:113
  1306.0 20.0 %collective-permute-start.1 = (bf16[64,128]{1,0:T(8,128)(2,1)S(1)}, bf16[64,128]{1,0:T(8,128)(2,1)S(1)}, u32[]{:S(2)}, u32[]{:S(2)}) collective-permute-start(bf16[64,128]{1,0:T(8,128)(2,1)S(1)} %get-tuple-element.1049), channel_id=1, source_target_pairs={{1,0},{2,1},{3,2},{4,3},{5,4},{6,5},{7,6},{8,7},{9,8},{10,9},{11,1... | collective-permute-start | bytes 49160 | tf_op jit(solution)/shard_map/while/body/eval_jaxpr/ppermute | solution.py:114
  1326.6 29.0 %collective-permute-start = (bf16[64,128]{1,0:T(8,128)(2,1)}, bf16[64,128]{1,0:T(8,128)(2,1)S(1)}, u32[]{:S(2)}, u32[]{:S(2)}) collective-permute-start(bf16[64,128]{1,0:T(8,128)(2,1)} %get-tuple-element.1044), channel_id=1, source_target_pairs={{0,1},{1,2},{2,3},{3,4},{4,5},{5,6},{6,7},{7,8},{8,9},{9,10},{10,1... | collective-permute-start | bytes 49160 | tf_op jit(solution)/shard_map/while/body/eval_jaxpr/ppermute | solution.py:113
  1356.3 29.0 %collective-permute-start = (bf16[64,128]{1,0:T(8,128)(2,1)}, bf16[64,128]{1,0:T(8,128)(2,1)S(1)}, u32[]{:S(2)}, u32[]{:S(2)}) collective-permute-start(bf16[64,128]{1,0:T(8,128)(2,1)} %get-tuple-element.1044), channel_id=1, source_target_pairs={{0,1},{1,2},{2,3},{3,4},{4,5},{5,6},{6,7},{7,8},{8,9},{9,10},{10,1... | collective-permute-start | bytes 49160 | tf_op jit(solution)/shard_map/while/body/eval_jaxpr/ppermute | solution.py:113
  1386.0 29.0 %collective-permute-start = (bf16[64,128]{1,0:T(8,128)(2,1)}, bf16[64,128]{1,0:T(8,128)(2,1)S(1)}, u32[]{:S(2)}, u32[]{:S(2)}) collective-permute-start(bf16[64,128]{1,0:T(8,128)(2,1)} %get-tuple-element.1044), channel_id=1, source_target_pairs={{0,1},{1,2},{2,3},{3,4},{4,5},{5,6},{6,7},{7,8},{8,9},{9,10},{10,1... | collective-permute-start | bytes 49160 | tf_op jit(solution)/shard_map/while/body/eval_jaxpr/ppermute | solution.py:113
  1415.7 29.0 %collective-permute-start = (bf16[64,128]{1,0:T(8,128)(2,1)}, bf16[64,128]{1,0:T(8,128)(2,1)S(1)}, u32[]{:S(2)}, u32[]{:S(2)}) collective-permute-start(bf16[64,128]{1,0:T(8,128)(2,1)} %get-tuple-element.1044), channel_id=1, source_target_pairs={{0,1},{1,2},{2,3},{3,4},{4,5},{5,6},{6,7},{7,8},{8,9},{9,10},{10,1... | collective-permute-start | bytes 49160 | tf_op jit(solution)/shard_map/while/body/eval_jaxpr/ppermute | solution.py:113
  1445.4 29.0 %collective-permute-start = (bf16[64,128]{1,0:T(8,128)(2,1)}, bf16[64,128]{1,0:T(8,128)(2,1)S(1)}, u32[]{:S(2)}, u32[]{:S(2)}) collective-permute-start(bf16[64,128]{1,0:T(8,128)(2,1)} %get-tuple-element.1044), channel_id=1, source_target_pairs={{0,1},{1,2},{2,3},{3,4},{4,5},{5,6},{6,7},{7,8},{8,9},{9,10},{10,1... | collective-permute-start | bytes 49160 | tf_op jit(solution)/shard_map/while/body/eval_jaxpr/ppermute | solution.py:113
  1475.1 29.0 %collective-permute-start = (bf16[64,128]{1,0:T(8,128)(2,1)}, bf16[64,128]{1,0:T(8,128)(2,1)S(1)}, u32[]{:S(2)}, u32[]{:S(2)}) collective-permute-start(bf16[64,128]{1,0:T(8,128)(2,1)} %get-tuple-element.1044), channel_id=1, source_target_pairs={{0,1},{1,2},{2,3},{3,4},{4,5},{5,6},{6,7},{7,8},{8,9},{9,10},{10,1... | collective-permute-start | bytes 49160 | tf_op jit(solution)/shard_map/while/body/eval_jaxpr/ppermute | solution.py:113
  1504.8 29.0 %collective-permute-start = (bf16[64,128]{1,0:T(8,128)(2,1)}, bf16[64,128]{1,0:T(8,128)(2,1)S(1)}, u32[]{:S(2)}, u32[]{:S(2)}) collective-permute-start(bf16[64,128]{1,0:T(8,128)(2,1)} %get-tuple-element.1044), channel_id=1, source_target_pairs={{0,1},{1,2},{2,3},{3,4},{4,5},{5,6},{6,7},{7,8},{8,9},{9,10},{10,1... | collective-permute-start | bytes 49160 | tf_op jit(solution)/shard_map/while/body/eval_jaxpr/ppermute | solution.py:113
  1534.5 18.5 %collective-permute-start = (bf16[64,128]{1,0:T(8,128)(2,1)}, bf16[64,128]{1,0:T(8,128)(2,1)S(1)}, u32[]{:S(2)}, u32[]{:S(2)}) collective-permute-start(bf16[64,128]{1,0:T(8,128)(2,1)} %get-tuple-element.1044), channel_id=1, source_target_pairs={{0,1},{1,2},{2,3},{3,4},{4,5},{5,6},{6,7},{7,8},{8,9},{9,10},{10,1... | collective-permute-start | bytes 49160 | tf_op jit(solution)/shard_map/while/body/eval_jaxpr/ppermute | solution.py:113
  (49 other events, 729.3 us)
Sparse Core Ops, SparseCore 0:
  1553.2 189.8 all-reduce.1
where the time goes:
time: 1770 us; the launch traced here: 1760 us
  starting transfers between devices  689 us (39%)
  other arithmetic  612 us (35%)
  waiting for transfers between devices  266 us (15%)
  local copies, waits for them, and re-layouts  114 us (6%)
  matrix products  29 us (2%)
  blocking collectives  28.6 us (2%)
    ppermute x46, starting transfers between devices, tick(): recv_act = lax.ppermute(y_out, 'stage', fwd_perm)  591 us
    scatter-add x46, other arithmetic, tick(): grad_emb = grad_emb.at[tok_b].add(emb_rows)  556 us
    psum x1, waiting for transfers between devices, device_fn(): grad_emb = lax.psum(final_state[7], 'stage')  161 us
    ppermute x46, waiting for transfers between devices, tick(): recv_grad = lax.ppermute(grad_in, 'stage', bwd_perm)  105 us
    ppermute x46, starting transfers between devices, tick(): recv_grad = lax.ppermute(grad_in, 'stage', bwd_perm)  97.8 us
    gather x16, local copies, waits for them, and re-layouts, tick(): x_in = jnp.where(is_first, jnp.take(emb_table, tok_f, axis=0), recv_act)  77.3 us
  transfers between devices with their start and end apart: 93, of which 15 were waited for; matrix products, arithmetic and copies ran while one was open for 34% of the time, Pallas kernels for 0%

commit v1 on v0

v1 whole, which is shorter than its diff:
```python
import functools
import math

import jax
import jax.numpy as jnp
from jax import lax
from jax.experimental import pallas as pl
from jax.experimental.pallas import tpu as pltpu
from jax.sharding import PartitionSpec as P

F32 = jnp.float32
BF16 = jnp.bfloat16
MESH = pl.DeviceIdType.MESH
LANES = 128
TILE = 16
HEAD_COLS = 1024
TABLE_ROWS = 512
GELU_C = math.sqrt(2.0 / math.pi)
GELU_K = 0.044715
RMS_EPS = 1e-6


def dot_nn(a, b):
    return lax.dot_general(a, b, (((1,), (0,)), ((), ())), preferred_element_type=F32)


def dot_nt(a, b):
    return lax.dot_general(a, b, (((1,), (1,)), ((), ())), preferred_element_type=F32)


def dot_tn(a, b):
    return lax.dot_general(a, b, (((0,), (0,)), ((), ())), preferred_element_type=F32)


def gelu(a):
    return a * (0.5 * (1.0 + jnp.tanh(GELU_C * (a + GELU_K * (a * a * a)))))


def gelu_grad(a):
    sq = a * a
    t = jnp.tanh(GELU_C * (a + GELU_K * (sq * a)))
    return 0.5 * (1.0 + t) + (0.5 * GELU_C) * a * (1.0 - t * t) * (1.0 + (3.0 * GELU_K) * sq)


def chunks(total, size):
    return size, total // size, total % size


def step_kernel(n_stage, inv_count, tok_ref, lab_ref, table_hbm, w_up_ref, w_down_ref,
                n_out, dx_out, misc_out, gup_out, gdown_out,
                table, up_all, down_all, x_hist, pre_hist, dy_hist, logits,
                n_mine, misc_mine, dx_mine, x_rows, n_all, misc_all, dx_all, x_all, dy_all,
                table_sem, up_recv, down_recv, up_send, down_send,
                x_recv, dy_recv, n_recv, misc_recv, dx_recv,
                x_send, dy_send, n_send, misc_send, dx_send):
    me = lax.axis_index("stage")
    dp = lax.axis_index("dp")
    n_chip = n_stage // 2
    half = n_chip // 2
    chip, core = me // 2, lax.rem(me, 2)
    dim = table.shape[2]
    vocab = table.shape[0] * TILE
    seq = x_hist.shape[1]
    logit_scale = dim ** -0.5

    def slot_at(offset, which):
        return lax.rem(chip + offset + n_chip, n_chip) * 2 + which

    right, left, partner = slot_at(1, core), slot_at(-1, core), chip * 2 + (1 - core)

    table_copy = pltpu.make_async_copy(table_hbm, table, table_sem)
    table_copy.start()

    barrier = pltpu.get_barrier_semaphore()

    def greet(k, carry):
        pl.semaphore_signal(barrier, inc=1, device_id=(dp, lax.rem(me + k, n_stage)), device_id_type=MESH)
        return carry

    lax.fori_loop(1, n_stage, greet, 0)
    pl.semaphore_wait(barrier, n_stage - 1)

    def up_copy(slot, way, target, own=False):
        return pltpu.make_async_remote_copy(
            src_ref=w_up_ref.at[0] if own else up_all.at[slot], dst_ref=up_all.at[slot],
            send_sem=up_send.at[way, slot], recv_sem=up_recv.at[slot],
            device_id=(dp, target), device_id_type=MESH)

    def down_copy(slot, way, target, own=False):
        return pltpu.make_async_remote_copy(
            src_ref=w_down_ref.at[0] if own else down_all.at[slot], dst_ref=down_all.at[slot],
            send_sem=down_send.at[way, slot], recv_sem=down_recv.at[slot],
            device_id=(dp, target), device_id_type=MESH)

    sends = []

    def send(copy):
        copy.start()
        sends.append(copy)

    for way, target in ((0, right), (1, left), (2, partner)):
        send(up_copy(me, way, target, own=True))
        send(down_copy(me, way, target, own=True))
    up_all[me] = w_up_ref[0]
    down_all[me] = w_down_ref[0]

    table_copy.wait()
    row_iota = lax.broadcasted_iota(jnp.int32, (TILE, dim), 0)

    def embed(i, carry):
        tok = tok_ref[me, i]
        tile = table[lax.div(tok, TILE)].astype(F32)
        row = jnp.sum(jnp.where(row_iota == lax.rem(tok, TILE), tile, 0.0), axis=0, keepdims=True)
        x_rows[pl.ds(i, 1), :] = row
        return carry

    lax.fori_loop(0, seq, embed, 0)
    x_now = x_rows[...].astype(BF16)

    for t in range(1, half + 1):
        slot_l, slot_r = slot_at(-t, core), slot_at(t, core)
        up_copy(slot_l, 0, right).wait_recv()
        if t < half:
            send(up_copy(slot_l, 0, right))
        send(up_copy(slot_l, 2, partner))
        down_copy(slot_r, 1, left).wait_recv()
        if t < half:
            send(down_copy(slot_r, 1, left))
        send(down_copy(slot_r, 2, partner))
        if t < half:
            down_copy(slot_l, 0, right).wait_recv()
            if t < half - 1:
                send(down_copy(slot_l, 0, right))
            send(down_copy(slot_l, 2, partner))
            up_copy(slot_r, 1, left).wait_recv()
            if t < half - 1:
                send(up_copy(slot_r, 1, left))
            send(up_copy(slot_r, 2, partner))

    for t in range(n_chip):
        slot = slot_at(t, 1 - core)
        up_copy(slot, 2, partner).wait_recv()
        down_copy(slot, 2, partner).wait_recv()

    def forward(s, x_act):
        x_hist[s] = x_act
        pre = dot_nn(x_act, up_all[s]).astype(BF16)
        pre_hist[s] = pre
        hidden = gelu(pre.astype(F32)).astype(BF16)
        return (x_act.astype(F32) + dot_nn(hidden, down_all[s])).astype(BF16)

    x_last = lax.fori_loop(0, n_stage, forward, x_now)

    def peer_copy(src, dst, send_sem, recv_sem, target):
        return pltpu.make_async_remote_copy(
            src_ref=src, dst_ref=dst.at[me], send_sem=send_sem.at[target], recv_sem=recv_sem.at[me],
            device_id=(dp, target), device_id_type=MESH)

    def x_copy(target):
        return peer_copy(x_hist.at[target], x_all, x_send, x_recv, target)

    def dy_copy(target):
        return peer_copy(dy_hist.at[target], dy_all, dy_send, dy_recv, target)

    def n_copy(target):
        return peer_copy(n_mine, n_all, n_send, n_recv, target)

    def misc_copy(target):
        return peer_copy(misc_mine, misc_all, misc_send, misc_recv, target)

    def dx_copy(target):
        return peer_copy(dx_mine, dx_all, dx_send, dx_recv, target)

    def to_peers(start):
        def one(k, carry):
            start(lax.rem(me + k, n_stage))
            return carry
        lax.fori_loop(1, n_stage, one, 0)

    x_wide = x_last.astype(F32)
    inv_rms = lax.rsqrt(jnp.mean(x_wide * x_wide, axis=-1, keepdims=True) + RMS_EPS)
    normed = (x_wide * inv_rms).astype(BF16)
    n_mine[...] = normed

    cols, n_full, tail = chunks(vocab, HEAD_COLS)

    def table_rows(first, width):
        tile = first // TILE if isinstance(first, int) else lax.div(first, TILE)
        return table[pl.ds(tile, width // TILE)].reshape(width, dim)

    def pass_one(first, width, carry):
        top, total = carry
        z = (dot_nt(normed, table_rows(first, width)) * logit_scale).astype(BF16)
        logits[:, pl.ds(first, width)] = z
        parts = [z[:, j:j + LANES].astype(F32) for j in range(0, width, LANES)]
        new_top = top
        for part in parts:
            new_top = jnp.maximum(new_top, part)
        total = total * jnp.exp(top - new_top)
        for part in parts:
            total = total + jnp.exp(part - new_top)
        return new_top, total

    def head_loop(body, carry):
        carry = lax.fori_loop(0, n_full, lambda i, c: body(pl.multiple_of(i * cols, cols), cols, c), carry)
        if tail:
            carry = body(n_full * cols, tail, carry)
        return carry

    top, total = head_loop(pass_one, (jnp.full((seq, LANES), -1e30, F32), jnp.zeros((seq, LANES), F32)))
    row_top = jnp.max(top, axis=-1, keepdims=True)
    row_sum = jnp.sum(total * jnp.exp(top - row_top), axis=-1, keepdims=True)
    lse = row_top + jnp.log(row_sum)

    to_peers(lambda target: x_copy(target).start())
    x_all[me] = x_hist[me]

    label = lab_ref[...]
    lane_iota = lax.broadcasted_iota(jnp.int32, (seq, LANES), 1)

    def pass_two(first, width, carry):
        picked, grad_n = carry
        base = label - first
        grads = []
        for j in range(0, width, LANES):
            z = logits[:, pl.ds(first + j, LANES)].astype(F32)
            prob = jnp.exp(z - lse)
            hit = lane_iota == base - j
            picked = picked + jnp.where(hit, z, 0.0)
            grads.append((jnp.where(hit, prob - 1.0, prob) * inv_count).astype(BF16))
        grad_z = jnp.concatenate(grads, axis=1)
        return picked, grad_n + dot_nn(grad_z, table_rows(first, width))

    picked, grad_n = head_loop(pass_two, (jnp.zeros((seq, LANES), F32), jnp.zeros((seq, dim), F32)))
    loss = jnp.sum((lse - jnp.sum(picked, axis=-1, keepdims=True)) * inv_count)
    eye = lax.broadcasted_iota(jnp.int32, (seq, LANES), 0) == lane_iota
    lse_row = jnp.sum(jnp.where(eye, lse, 0.0), axis=0, keepdims=True)
    row8 = lax.broadcasted_iota(jnp.int32, (8, LANES), 0)
    misc = jnp.where(row8 == 0, jnp.broadcast_to(lse_row, (8, LANES)), loss)
    misc_mine[...] = misc
    n_all[me] = normed
    misc_all[me] = misc

    grad_n = (grad_n * logit_scale).astype(BF16).astype(F32)
    along = jnp.mean(grad_n * x_wide, axis=-1, keepdims=True)
    grad_x = (inv_rms * grad_n - x_wide * (inv_rms * inv_rms * inv_rms * along)).astype(BF16)

    def backward(k, grad_out):
        s = n_stage - 1 - k
        dy_hist[s] = grad_out
        grad_hidden = dot_nt(grad_out, down_all[s]).astype(BF16).astype(F32)
        grad_pre = (grad_hidden * gelu_grad(pre_hist[s].astype(F32))).astype(BF16)
        result = (grad_out.astype(F32) + dot_nt(grad_pre, up_all[s])).astype(BF16)

        @pl.when(s != me)
        def _():
            dy_copy(s).start()

        return result

    to_peers(lambda target: n_copy(target).start())
    grad_in = lax.fori_loop(0, n_stage, backward, grad_x)
    dx_mine[...] = grad_in
    to_peers(lambda target: misc_copy(target).start())
    dy_all[me] = dy_hist[me]
    dx_all[me] = grad_in

    to_peers(lambda target: x_copy(target).wait_send())

    def wait_from(buf, recv):
        def one(k, carry):
            source = lax.rem(me + k, n_stage)
            pltpu.make_async_remote_copy(
                src_ref=buf.at[source], dst_ref=buf.at[source], send_sem=dx_send.at[source], recv_sem=recv.at[source],
                device_id=(dp, source), device_id_type=MESH).wait_recv()
            return carry
        lax.fori_loop(1, n_stage, one, 0)

    wait_from(x_all, x_recv)
    to_peers(lambda target: dx_copy(target).start())
    wait_from(dy_all, dy_recv)
    up, down = w_up_ref[0], w_down_ref[0]
    gup_out[...] = jnp.zeros_like(gup_out)
    gdown_out[...] = jnp.zeros_like(gdown_out)
    group = max(1, 256 // seq)

    def wgrad(i, carry):
        x_act = x_all[pl.ds(i * group, group)].reshape(group * seq, dim)
        grad_out = dy_all[pl.ds(i * group, group)].reshape(group * seq, dim)
        pre = dot_nn(x_act, up).astype(BF16).astype(F32)
        hidden = gelu(pre).astype(BF16)
        gdown_out[...] += dot_tn(hidden, grad_out)
        grad_hidden = dot_nt(grad_out, down).astype(BF16).astype(F32)
        grad_pre = (grad_hidden * gelu_grad(pre)).astype(BF16)
        gup_out[...] += dot_tn(x_act, grad_pre)
        return carry

    lax.fori_loop(0, n_stage // group, wgrad, 0)

    wait_from(n_all, n_recv)
    wait_from(misc_all, misc_recv)
    wait_from(dx_all, dx_recv)
    n_out[...] = n_all[...]
    misc_out[...] = misc_all[...]
    dx_out[...] = dx_all[...]

    for copy in sends:
        copy.wait_send()
    for make in (dy_copy, n_copy, misc_copy, dx_copy):
        to_peers(lambda target, make=make: make(target).wait_send())


def table_kernel(inv_count, tok_ref, lse_ref, lab_ref, n_ref, dx_ref, table_hbm, out_hbm,
                 table, acc, dx_wide, table_sem, out_sem):
    vocab, dim = table.shape
    count = n_ref.shape[0]
    logit_scale = dim ** -0.5
    table_copy = pltpu.make_async_copy(table_hbm, table, table_sem)
    table_copy.start()
    acc[...] = jnp.zeros_like(acc)
    dx_wide[...] = dx_ref[...].astype(F32)

    def scatter(i, carry):
        tok = tok_ref[0, i]
        acc[pl.ds(tok, 1), :] += dx_wide[pl.ds(i, 1), :]
        return carry

    lax.fori_loop(0, count, scatter, 0, unroll=8)
    table_copy.wait()

    rows, n_full, tail = chunks(vocab, TABLE_ROWS)
    lse = lse_ref[...]
    label = lab_ref[...]

    def out_copy(first, height, index):
        return pltpu.make_async_copy(acc.at[pl.ds(first, height), :], out_hbm.at[pl.ds(first, height), :], out_sem.at[index])

    def part(first, height, index):
        z = (dot_nt(table[pl.ds(first, height), :], n_ref[...]) * logit_scale).astype(BF16).astype(F32)
        prob = jnp.exp(z - lse)
        row_iota = lax.broadcasted_iota(jnp.int32, (height, count), 0)
        hit = row_iota == label - first
        grad_z = (jnp.where(hit, prob - 1.0, prob) * inv_count).astype(BF16)
        acc[pl.ds(first, height), :] += dot_nn(grad_z, n_ref[...]) * logit_scale
        out_copy(first, height, index).start()

    def loop(i, carry):
        part(pl.multiple_of(i * rows, rows), rows, i)
        return carry

    lax.fori_loop(0, n_full, loop, 0)
    if tail:
        part(n_full * rows, tail, n_full)

    def drain(i, carry):
        out_copy(pl.multiple_of(i * rows, rows), rows, i).wait()
        return carry

    lax.fori_loop(0, n_full, drain, 0)
    if tail:
        out_copy(n_full * rows, tail, n_full).wait()


def solution(mesh):
    n_stage = mesh.shape["stage"]

    def device_fn(tokens, labels, emb_table, w_up, w_down):
        n_micro, seq = tokens.shape
        vocab, dim = emb_table.shape
        ffn = w_up.shape[2]
        count = n_micro * seq
        inv_count = 1.0 / count
        stage = lax.axis_index("stage")
        label_col = lax.dynamic_index_in_dim(labels, stage, 0, keepdims=False).reshape(seq, 1)
        vmem = pl.BlockSpec(memory_space=pltpu.VMEM)
        smem = pl.BlockSpec(memory_space=pltpu.SMEM)
        hbm = pl.BlockSpec(memory_space=pl.ANY)
        dma = pltpu.SemaphoreType.DMA

        n_all, dx_all, misc, g_up, g_down = pl.pallas_call(
            functools.partial(step_kernel, n_stage, inv_count),
            name="step",
            out_shape=(
                jax.ShapeDtypeStruct((n_stage, seq, dim), BF16),
                jax.ShapeDtypeStruct((n_stage, seq, dim), BF16),
                jax.ShapeDtypeStruct((n_stage, 8, LANES), F32),
                jax.ShapeDtypeStruct((dim, ffn), F32),
                jax.ShapeDtypeStruct((ffn, dim), F32),
            ),
            in_specs=[smem, vmem, hbm, vmem, vmem],
            out_specs=(vmem,) * 5,
            scratch_shapes=[
                pltpu.VMEM((vocab // TILE, TILE, dim), BF16),
                pltpu.VMEM((n_stage, dim, ffn), BF16),
                pltpu.VMEM((n_stage, ffn, dim), BF16),
                pltpu.VMEM((n_stage, seq, dim), BF16),
                pltpu.VMEM((n_stage, seq, ffn), BF16),
                pltpu.VMEM((n_stage, seq, dim), BF16),
                pltpu.VMEM((seq, vocab), BF16),
                pltpu.VMEM((seq, dim), BF16),
                pltpu.VMEM((8, LANES), F32),
                pltpu.VMEM((seq, dim), BF16),
                pltpu.VMEM((seq, dim), F32),
                pltpu.VMEM((n_stage, seq, dim), BF16),
                pltpu.VMEM((n_stage, 8, LANES), F32),
                pltpu.VMEM((n_stage, seq, dim), BF16),
                pltpu.VMEM((n_stage, seq, dim), BF16),
                pltpu.VMEM((n_stage, seq, dim), BF16),
                dma, dma((n_stage,)), dma((n_stage,)), dma((3, n_stage)), dma((3, n_stage)),
                dma((n_stage,)), dma((n_stage,)), dma((n_stage,)), dma((n_stage,)), dma((n_stage,)),
                dma((n_stage,)), dma((n_stage,)), dma((n_stage,)), dma((n_stage,)), dma((n_stage,)),
            ],
            compiler_params=pltpu.CompilerParams(collective_id=0, has_side_effects=True),
        )(tokens, label_col, emb_table.reshape(vocab // TILE, TILE, dim), w_up, w_down)

        n_parts = -(-vocab // TABLE_ROWS)
        grad_emb = pl.pallas_call(
            functools.partial(table_kernel, inv_count),
            name="table_grad",
            out_shape=jax.ShapeDtypeStruct((vocab, dim), F32),
            in_specs=[smem, vmem, vmem, vmem, vmem, hbm],
            out_specs=hbm,
            scratch_shapes=[
                pltpu.VMEM((vocab, dim), BF16),
                pltpu.VMEM((vocab, dim), F32),
                pltpu.VMEM((count, dim), F32),
                dma, dma((n_parts,)),
            ],
        )(tokens.reshape(1, count), misc[:, 0, :seq].reshape(1, count), labels.reshape(1, count),
          n_all.reshape(count, dim), dx_all.reshape(count, dim), emb_table)
        loss = jnp.sum(misc[:, 1, 0]).reshape(1)
        return loss, g_up[None], g_down[None], grad_emb

    return jax.shard_map(device_fn, mesh=mesh, in_specs=(P("dp", None), P("dp", None), P(None, None), P("stage", None, None), P("stage", None, None)), out_specs=(P("dp"), P(("dp", "stage"), None, None), P(("dp", "stage"), None, None), P("dp", None)), check_vma=False)
```

time: 1770 us -> 159 us (0.09)
  starting transfers between devices: 689 us -> 0 us
  other arithmetic: 612 us -> 1.52 us
  waiting for transfers between devices: 266 us -> 0 us
  Pallas kernels: 0 us -> 149 us
  local copies, waits for them, and re-layouts: 114 us -> 7.08 us
  matrix products: 29 us -> 0 us
  blocking collectives: 28.6 us -> 0 us
    ppermute x92 -> x0, starting transfers between devices: 689 us -> none  [the longest x46 591 us: tick(): recv_act = lax.ppermute(y_out, 'stage', fwd_perm)]
    scatter-add x46 -> x0, other arithmetic: 556 us -> none  [tick(): grad_emb = grad_emb.at[tok_b].add(emb_rows)]
    psum x1 -> x0, waiting for transfers between devices: 161 us -> none  [device_fn(): grad_emb = lax.psum(final_state[7], 'stage')]
    pallas_call x0 -> x2, Pallas kernels: none -> 149 us  [the longest x1 82.4 us: device_fn(): pl.pallas_call(functools.partial(step_kernel, n_stage, inv_count), name='...]
    ppermute x92 -> x0, waiting for transfers between devices: 105 us -> none  [the longest x46 105 us: tick(): recv_grad = lax.ppermute(grad_in, 'stage', bwd_perm)]
    gather x16 -> x0, local copies, waits for them, and re-layouts: 77.3 us -> none  [tick(): x_in = jnp.where(is_first, jnp.take(emb_table, tok_f, axis=0), recv_act)]
    select_n x78 -> x0, other arithmetic: 43.5 us -> none  [the longest x46 32.2 us: tick(): grad_emb = grad_emb.at[tok_b].add(emb_rows)]
    dot_general x96 -> x0, matrix products: 29 us -> none  [the longest x16 12.8 us: block_forward(): branch = jnp.dot(hidden, w_down, preferred_element_type=jnp.float32)]
  transfers between devices with their start and end apart: 93 -> 0, of which waited for: 15 -> 0; matrix products, arithmetic and copies ran while one was open for 34% -> 0% of each run, Pallas kernels for 0% -> 0%
where the time goes in v1:
time: 159 us
  Pallas kernels  149 us (94%)
  local copies, waits for them, and re-layouts  7.08 us (4%)
    pallas_call x1, Pallas kernels, device_fn(): pl.pallas_call(functools.partial(step_kernel, n_stage, inv_count), name='...  82.4 us
    pallas_call x1, Pallas kernels, device_fn(): pl.pallas_call(functools.partial(table_kernel, inv_count), name='table_gr...  66.9 us

profile of v1, /device:TPU:21, one launch (start us, length us, event | category | flops | bytes accessed | tf_op | source)
XLA Modules:
  0.0 158.6 jit_solution(14529961015001603916)
XLA Ops:
  0.6 0.7 dynamic-slice_bitcast_fusion
  1.3 1.4 reshape.33.tok_ref
  2.7 1.4 reshape.34.lab_ref
  4.1 0.7 copy.9.lab_ref
  4.8 82.4 %step.1 = (bf16[16,64,128]{2,1,0:T(8,128)(2,1)}, bf16[16,64,128]{2,1,0:T(8,128)(2,1)}, f32[16,8,128]{2,1,0:T(8,128)}, f32[128,512]{1,0:T(8,128)}, f32[512,128]{1,0:T(8,128)}) custom-call(s32[16,64]{1,0:T(8,128)} %tok_ref.1, s32[64,1]{1,0:T(8,128)} %copy.9.lab_ref, bf16[1912,16,128]{2,1,0:T(8,128)(2,1)} %bitcast.8, bf16[1,128,512]{2,1,0:T(8,128)(2,1)} %w_up_ref.1, ...), custom_call_target="tpu_custom_call" | custom-call | tf_op jit(solution)/shard_map/step/pallas_call | solution.py:380
  87.2 0.0 copy-start.1
  87.2 0.0 copy-start
  87.2 1.5 slice_reduce_fusion.1
  88.7 0.9 slice_reduce_fusion
  89.6 0.7 reshape_squeeze.3.lse_ref
  90.3 66.9 %table_grad.1 = f32[30592,128]{1,0:T(8,128)} custom-call(s32[1,1024]{1,0:T(1,128)} %reshape.33.tok_ref, f32[1,1024]{1,0:T(1,128)} %reshape_squeeze.3.lse_ref, s32[1,1024]{1,0:T(1,128)} %reshape.34.lab_ref, bf16[1024,128]{1,0:T(8,128)(2,1)} %bitcast.9, bf16[1024,128]{1,0:T(8,128)(2,1)} %bitcast.10, bf16[30592,128]{1,0:T(8,128)(2,1)} %table_hbm.1), custom_call_target="tpu_custom_call" | custom-call | tf_op jit(solution)/shard_map/table_grad/pallas_call | solution.py:417
  157.2 0.0 copy-done.1
  157.2 0.7 copy.12
  157.9 0.0 copy-done
  157.9 0.7 copy.13
Async XLA Ops:
  87.2 70.0 %copy-start.1 = (f32[128,512]{1,0:T(8,128)S(1)}, f32[128,512]{1,0:T(8,128)}, u32[]{:S(2)}) copy-start(f32[128,512]{1,0:T(8,128)} %get-tuple-element.10) | copy-start | bytes 786436
  87.2 70.7 %copy-start = (f32[512,128]{1,0:T(8,128)S(1)}, f32[512,128]{1,0:T(8,128)}, u32[]{:S(2)}) copy-start(f32[512,128]{1,0:T(8,128)} %get-tuple-element.11) | copy-start | bytes 786436

commit v2 on v1

--- a/solution.py
+++ b/solution.py
@@ -14,7 +14,7 @@
 LANES = 128
 TILE = 16
 HEAD_COLS = 1024
-TABLE_ROWS = 512
+TABLE_ROWS = 2048
 GELU_C = math.sqrt(2.0 / math.pi)
 GELU_K = 0.044715
 RMS_EPS = 1e-6
@@ -47,7 +47,7 @@
 
 
 def step_kernel(n_stage, inv_count, tok_ref, lab_ref, table_hbm, w_up_ref, w_down_ref,
-                n_out, dx_out, misc_out, gup_out, gdown_out,
+                n_out, dx_out, x_out, dy_out, misc_out,
                 table, up_all, down_all, x_hist, pre_hist, dy_hist, logits,
                 n_mine, misc_mine, dx_mine, x_rows, n_all, misc_all, dx_all, x_all, dy_all,
                 table_sem, up_recv, down_recv, up_send, down_send,
@@ -215,28 +215,37 @@
     to_peers(lambda target: x_copy(target).start())
     x_all[me] = x_hist[me]
 
-    label = lab_ref[...]
     lane_iota = lax.broadcasted_iota(jnp.int32, (seq, LANES), 1)
+    lane_wide = lane_iota.astype(F32)
+    square = lax.broadcasted_iota(jnp.int32, (seq, seq), 0) == lax.broadcasted_iota(jnp.int32, (seq, seq), 1)
+    label = jnp.sum(jnp.where(square, lab_ref[pl.ds(me, 1), :].astype(F32), 0.0), axis=-1, keepdims=True)
+    lse_count = lse + math.log(1.0 / inv_count)
 
     def pass_two(first, width, carry):
         picked, grad_n = carry
-        base = label - first
+        base = label - jnp.asarray(first, jnp.int32).astype(F32)
         grads = []
         for j in range(0, width, LANES):
             z = logits[:, pl.ds(first + j, LANES)].astype(F32)
-            prob = jnp.exp(z - lse)
-            hit = lane_iota == base - j
+            prob = jnp.exp(z - lse_count)
+            hit = lane_wide == base - float(j)
             picked = picked + jnp.where(hit, z, 0.0)
-            grads.append((jnp.where(hit, prob - 1.0, prob) * inv_count).astype(BF16))
+            grads.append(jnp.where(hit, prob - inv_count, prob).astype(BF16))
         grad_z = jnp.concatenate(grads, axis=1)
         return picked, grad_n + dot_nn(grad_z, table_rows(first, width))
 
     picked, grad_n = head_loop(pass_two, (jnp.zeros((seq, LANES), F32), jnp.zeros((seq, dim), F32)))
-    loss = jnp.sum((lse - jnp.sum(picked, axis=-1, keepdims=True)) * inv_count)
+    picked = jnp.sum(picked, axis=-1, keepdims=True)
+    loss = jnp.sum((lse - picked) * inv_count)
+    label_prob = jnp.exp(picked - lse_count)
+    fix = (label_prob - inv_count).astype(BF16).astype(F32) - label_prob.astype(BF16).astype(F32)
     eye = lax.broadcasted_iota(jnp.int32, (seq, LANES), 0) == lane_iota
-    lse_row = jnp.sum(jnp.where(eye, lse, 0.0), axis=0, keepdims=True)
+
+    def as_row(column):
+        return jnp.broadcast_to(jnp.sum(jnp.where(eye, column, 0.0), axis=0, keepdims=True), (8, LANES))
+
     row8 = lax.broadcasted_iota(jnp.int32, (8, LANES), 0)
-    misc = jnp.where(row8 == 0, jnp.broadcast_to(lse_row, (8, LANES)), loss)
+    misc = jnp.where(row8 == 0, as_row(lse_count), jnp.where(row8 == 1, as_row(fix), loss))
     misc_mine[...] = misc
     n_all[me] = normed
     misc_all[me] = misc
@@ -279,14 +288,39 @@
     wait_from(x_all, x_recv)
     to_peers(lambda target: dx_copy(target).start())
     wait_from(dy_all, dy_recv)
-    up, down = w_up_ref[0], w_down_ref[0]
+    wait_from(n_all, n_recv)
+    wait_from(misc_all, misc_recv)
+    wait_from(dx_all, dx_recv)
+    n_out[...] = n_all[...]
+    misc_out[...] = misc_all[...]
+    dx_out[...] = dx_all[...]
+    x_out[...] = x_all[...]
+    dy_out[...] = dy_all[...]
+
+    for copy in sends:
+        copy.wait_send()
+    for make in (dy_copy, n_copy, misc_copy, dx_copy):
+        to_peers(lambda target, make=make: make(target).wait_send())
+
+
+def table_kernel(inv_count, tok_ref, lab_ref, misc_ref, n_ref, dx_ref, x_ref, dy_ref, up_ref, down_ref, table_hbm,
+                 out_hbm, loss_out, gup_out, gdown_out, table, acc, dx_wide, fix_rows, lse_row, table_sem, out_sem):
+    vocab, dim = table.shape
+    n_micro, seq, _ = n_ref.shape
+    count = n_micro * seq
+    logit_scale = dim ** -0.5
+    table_copy = pltpu.make_async_copy(table_hbm, table, table_sem)
+    table_copy.start()
+    acc[...] = jnp.zeros_like(acc)
+
+    up, down = up_ref[0], down_ref[0]
     gup_out[...] = jnp.zeros_like(gup_out)
     gdown_out[...] = jnp.zeros_like(gdown_out)
     group = max(1, 256 // seq)
 
     def wgrad(i, carry):
-        x_act = x_all[pl.ds(i * group, group)].reshape(group * seq, dim)
-        grad_out = dy_all[pl.ds(i * group, group)].reshape(group * seq, dim)
+        x_act = x_ref[pl.ds(i * group, group)].reshape(group * seq, dim)
+        grad_out = dy_ref[pl.ds(i * group, group)].reshape(group * seq, dim)
         pre = dot_nn(x_act, up).astype(BF16).astype(F32)
         hidden = gelu(pre).astype(BF16)
         gdown_out[...] += dot_tn(hidden, grad_out)
@@ -295,53 +329,45 @@
         gup_out[...] += dot_tn(x_act, grad_pre)
         return carry
 
-    lax.fori_loop(0, n_stage // group, wgrad, 0)
-
-    wait_from(n_all, n_recv)
-    wait_from(misc_all, misc_recv)
-    wait_from(dx_all, dx_recv)
-    n_out[...] = n_all[...]
-    misc_out[...] = misc_all[...]
-    dx_out[...] = dx_all[...]
-
-    for copy in sends:
-        copy.wait_send()
-    for make in (dy_copy, n_copy, misc_copy, dx_copy):
-        to_peers(lambda target, make=make: make(target).wait_send())
-
-
-def table_kernel(inv_count, tok_ref, lse_ref, lab_ref, n_ref, dx_ref, table_hbm, out_hbm,
-                 table, acc, dx_wide, table_sem, out_sem):
-    vocab, dim = table.shape
-    count = n_ref.shape[0]
-    logit_scale = dim ** -0.5
-    table_copy = pltpu.make_async_copy(table_hbm, table, table_sem)
-    table_copy.start()
-    acc[...] = jnp.zeros_like(acc)
-    dx_wide[...] = dx_ref[...].astype(F32)
-
-    def scatter(i, carry):
-        tok = tok_ref[0, i]
-        acc[pl.ds(tok, 1), :] += dx_wide[pl.ds(i, 1), :]
-        return carry
-
-    lax.fori_loop(0, count, scatter, 0, unroll=8)
+    lax.fori_loop(0, n_micro // group, wgrad, 0)
+
+    eye = lax.broadcasted_iota(jnp.int32, (seq, LANES), 0) == lax.broadcasted_iota(jnp.int32, (seq, LANES), 1)
+    per_row = LANES // seq
+    total = jnp.zeros((8, LANES), F32)
+    for m in range(n_micro):
+        misc = misc_ref[m]
+        total = total + misc
+        fix = jnp.sum(jnp.where(eye, misc[1:2, :], 0.0), axis=-1, keepdims=True) * logit_scale
+        fix_rows[pl.ds(m * seq, seq), :] = n_ref[m].astype(F32) * fix
+        dx_wide[pl.ds(m * seq, seq), :] = dx_ref[m].astype(F32)
+        if m % per_row == 0:
+            row = misc
+            for k in range(1, per_row):
+                row = row + pltpu.roll(misc_ref[m + k], k * seq, 1)
+            lse_row[:, pl.ds(m * seq, LANES)] = row
+    loss_out[0] = jnp.max(total[2:3, :])
+
+    def scatter(m, carry):
+        def one(i, inner):
+            acc[pl.ds(tok_ref[m, i], 1), :] += dx_wide[pl.ds(m * seq + i, 1), :]
+            acc[pl.ds(lab_ref[m, i], 1), :] += fix_rows[pl.ds(m * seq + i, 1), :]
+            return inner
+        return lax.fori_loop(0, seq, one, carry, unroll=8)
+
+    lax.fori_loop(0, n_micro, scatter, 0)
     table_copy.wait()
 
     rows, n_full, tail = chunks(vocab, TABLE_ROWS)
-    lse = lse_ref[...]
-    label = lab_ref[...]
+    lse = lse_row[0:1, :]
 
     def out_copy(first, height, index):
         return pltpu.make_async_copy(acc.at[pl.ds(first, height), :], out_hbm.at[pl.ds(first, height), :], out_sem.at[index])
 
     def part(first, height, index):
-        z = (dot_nt(table[pl.ds(first, height), :], n_ref[...]) * logit_scale).astype(BF16).astype(F32)
-        prob = jnp.exp(z - lse)
-        row_iota = lax.broadcasted_iota(jnp.int32, (height, count), 0)
-        hit = row_iota == label - first
-        grad_z = (jnp.where(hit, prob - 1.0, prob) * inv_count).astype(BF16)
-        acc[pl.ds(first, height), :] += dot_nn(grad_z, n_ref[...]) * logit_scale
+        normed = n_ref[...].reshape(count, dim)
+        z = (dot_nt(table[pl.ds(first, height), :], normed) * logit_scale).astype(BF16).astype(F32)
+        grad_z = jnp.exp(z - lse).astype(BF16)
+        acc[pl.ds(first, height), :] += dot_nn(grad_z, normed) * logit_scale
         out_copy(first, height, index).start()
 
     def loop(i, carry):
@@ -370,23 +396,16 @@
         ffn = w_up.shape[2]
         count = n_micro * seq
         inv_count = 1.0 / count
-        stage = lax.axis_index("stage")
-        label_col = lax.dynamic_index_in_dim(labels, stage, 0, keepdims=False).reshape(seq, 1)
         vmem = pl.BlockSpec(memory_space=pltpu.VMEM)
         smem = pl.BlockSpec(memory_space=pltpu.SMEM)
         hbm = pl.BlockSpec(memory_space=pl.ANY)
         dma = pltpu.SemaphoreType.DMA
 
-        n_all, dx_all, misc, g_up, g_down = pl.pallas_call(
+        act = jax.ShapeDtypeStruct((n_stage, seq, dim), BF16)
+        n_all, dx_all, x_all, dy_all, misc = pl.pallas_call(
             functools.partial(step_kernel, n_stage, inv_count),
             name="step",
-            out_shape=(
-                jax.ShapeDtypeStruct((n_stage, seq, dim), BF16),
-                jax.ShapeDtypeStruct((n_stage, seq, dim), BF16),
-                jax.ShapeDtypeStruct((n_stage, 8, LANES), F32),
-                jax.ShapeDtypeStruct((dim, ffn), F32),
-                jax.ShapeDtypeStruct((ffn, dim), F32),
-            ),
+            out_shape=(act, act, act, act, jax.ShapeDtypeStruct((n_stage, 8, LANES), F32)),
             in_specs=[smem, vmem, hbm, vmem, vmem],
             out_specs=(vmem,) * 5,
             scratch_shapes=[
@@ -411,24 +430,29 @@
                 dma((n_stage,)), dma((n_stage,)), dma((n_stage,)), dma((n_stage,)), dma((n_stage,)),
             ],
             compiler_params=pltpu.CompilerParams(collective_id=0, has_side_effects=True),
-        )(tokens, label_col, emb_table.reshape(vocab // TILE, TILE, dim), w_up, w_down)
+        )(tokens, labels, emb_table.reshape(vocab // TILE, TILE, dim), w_up, w_down)
 
         n_parts = -(-vocab // TABLE_ROWS)
-        grad_emb = pl.pallas_call(
+        grad_emb, loss, g_up, g_down = pl.pallas_call(
             functools.partial(table_kernel, inv_count),
             name="table_grad",
-            out_shape=jax.ShapeDtypeStruct((vocab, dim), F32),
-            in_specs=[smem, vmem, vmem, vmem, vmem, hbm],
-            out_specs=hbm,
+            out_shape=(
+                jax.ShapeDtypeStruct((vocab, dim), F32),
+                jax.ShapeDtypeStruct((1,), F32),
+                jax.ShapeDtypeStruct((dim, ffn), F32),
+                jax.ShapeDtypeStruct((ffn, dim), F32),
+            ),
+            in_specs=[smem, smem, vmem, vmem, vmem, vmem, vmem, vmem, vmem, hbm],
+            out_specs=(hbm, smem, vmem, vmem),
             scratch_shapes=[
                 pltpu.VMEM((vocab, dim), BF16),
                 pltpu.VMEM((vocab, dim), F32),
                 pltpu.VMEM((count, dim), F32),
+                pltpu.VMEM((count, dim), F32),
+                pltpu.VMEM((8, count), F32),
                 dma, dma((n_parts,)),
             ],
-        )(tokens.reshape(1, count), misc[:, 0, :seq].reshape(1, count), labels.reshape(1, count),
-          n_all.reshape(count, dim), dx_all.reshape(count, dim), emb_table)
-        loss = jnp.sum(misc[:, 1, 0]).reshape(1)
+        )(tokens, labels, misc, n_all, dx_all, x_all, dy_all, w_up, w_down, emb_table)
         return loss, g_up[None], g_down[None], grad_emb
 
     return jax.shard_map(device_fn, mesh=mesh, in_specs=(P("dp", None), P("dp", None), P(None, None), P("stage", None, None), P("stage", None, None)), out_specs=(P("dp"), P(("dp", "stage"), None, None), P(("dp", "stage"), None, None), P("dp", None)), check_vma=False)

time: 159 us -> 136 us (0.86)
  Pallas kernels: 149 us -> 135 us
  local copies, waits for them, and re-layouts: 7.08 us -> 0 us
    pallas_call x1, Pallas kernels: 66.9 us -> 53.4 us  [device_fn(): pl.pallas_call(functools.partial(table_kernel, inv_count), name='table_gr...]
    reshape x4 -> x0, local copies, waits for them, and re-layouts: 4.13 us -> none  [the longest x2 1.4 us: device_fn(): lax.dynamic_index_in_dim(labels, stage, 0, keepdims=False).reshape(seq, 1)]
where the time goes in v2:
time: 136 us
  Pallas kernels  135 us (99%)
    pallas_call x1, Pallas kernels, device_fn(): pl.pallas_call(functools.partial(step_kernel, n_stage, inv_count), name='...  81.9 us
    pallas_call x1, Pallas kernels, device_fn(): pl.pallas_call(functools.partial(table_kernel, inv_count), name='table_gr...  53.4 us

profile of v2, /device:TPU:21, one launch (start us, length us, event | category | flops | bytes accessed | tf_op | source)
XLA Modules:
  0.0 135.9 jit_solution(16682380228904790291)
XLA Ops:
  0.6 81.9 %step.1 = (bf16[16,64,128]{2,1,0:T(8,128)(2,1)}, bf16[16,64,128]{2,1,0:T(8,128)(2,1)}, bf16[16,64,128]{2,1,0:T(8,128)(2,1)}, bf16[16,64,128]{2,1,0:T(8,128)(2,1)}, f32[16,8,128]{2,1,0:T(8,128)}) custom-call(s32[16,64]{1,0:T(8,128)} %tok_ref.3, s32[16,64]{1,0:T(8,128)} %lab_ref.3, bf16[1912,16,128]{2,1,0:T(8,128)(2,1)} %bitcast.3, ...), custom_call_target="tpu_custom_call" | custom-call | tf_op jit(solution)/shard_map/step/pallas_call | solution.py:405
  82.6 53.4 %table_grad.1 = (f32[30592,128]{1,0:T(8,128)}, f32[1]{0:T(128)}, f32[128,512]{1,0:T(8,128)}, f32[512,128]{1,0:T(8,128)}) custom-call(s32[16,64]{1,0:T(8,128)} %tok_ref.3, s32[16,64]{1,0:T(8,128)} %lab_ref.3, f32[16,8,128]{2,1,0:T(8,128)} %get-tuple-element.13.misc_ref, bf16[16,64,128]{2,1,0:T(8,128)(2,1)} %get-tuple-element.14.n_ref, ...), custom_call_target="tpu_custom_call" | custom-call | tf_op jit(solution)/shard_map/table_grad/pallas_call | solution.py:436

commit v3 on v2

--- a/solution.py
+++ b/solution.py
@@ -15,6 +15,7 @@
 TILE = 16
 HEAD_COLS = 1024
 TABLE_ROWS = 2048
+OUT_ROWS = 2048
 GELU_C = math.sqrt(2.0 / math.pi)
 GELU_K = 0.044715
 RMS_EPS = 1e-6
@@ -47,12 +48,12 @@
 
 
 def step_kernel(n_stage, inv_count, tok_ref, lab_ref, table_hbm, w_up_ref, w_down_ref,
-                n_out, dx_out, x_out, dy_out, misc_out,
+                n_out, dx_out, x_out, dy_out, misc_out, head_hbm,
                 table, up_all, down_all, x_hist, pre_hist, dy_hist, logits,
-                n_mine, misc_mine, dx_mine, x_rows, n_all, misc_all, dx_all, x_all, dy_all,
+                n_mine, misc_mine, dx_mine, x_rows, lse_row, head_part, n_all, misc_all, dx_all, x_all, dy_all,
                 table_sem, up_recv, down_recv, up_send, down_send,
                 x_recv, dy_recv, n_recv, misc_recv, dx_recv,
-                x_send, dy_send, n_send, misc_send, dx_send):
+                x_send, dy_send, n_send, misc_send, dx_send, keep_sem, part_send, part_recv):
     me = lax.axis_index("stage")
     dp = lax.axis_index("dp")
     n_chip = n_stage // 2
@@ -177,10 +178,23 @@
             return carry
         lax.fori_loop(1, n_stage, one, 0)
 
+    def wait_from(buf, recv):
+        def one(k, carry):
+            source = lax.rem(me + k, n_stage)
+            pltpu.make_async_remote_copy(
+                src_ref=buf.at[source], dst_ref=buf.at[source], send_sem=dx_send.at[source], recv_sem=recv.at[source],
+                device_id=(dp, source), device_id_type=MESH).wait_recv()
+            return carry
+        lax.fori_loop(1, n_stage, one, 0)
+
     x_wide = x_last.astype(F32)
     inv_rms = lax.rsqrt(jnp.mean(x_wide * x_wide, axis=-1, keepdims=True) + RMS_EPS)
     normed = (x_wide * inv_rms).astype(BF16)
     n_mine[...] = normed
+    n_all[me] = normed
+    to_peers(lambda target: x_copy(target).start())
+    x_all[me] = x_hist[me]
+    to_peers(lambda target: n_copy(target).start())
 
     cols, n_full, tail = chunks(vocab, HEAD_COLS)
 
@@ -212,9 +226,6 @@
     row_sum = jnp.sum(total * jnp.exp(top - row_top), axis=-1, keepdims=True)
     lse = row_top + jnp.log(row_sum)
 
-    to_peers(lambda target: x_copy(target).start())
-    x_all[me] = x_hist[me]
-
     lane_iota = lax.broadcasted_iota(jnp.int32, (seq, LANES), 1)
     lane_wide = lane_iota.astype(F32)
     square = lax.broadcasted_iota(jnp.int32, (seq, seq), 0) == lax.broadcasted_iota(jnp.int32, (seq, seq), 1)
@@ -247,12 +258,13 @@
     row8 = lax.broadcasted_iota(jnp.int32, (8, LANES), 0)
     misc = jnp.where(row8 == 0, as_row(lse_count), jnp.where(row8 == 1, as_row(fix), loss))
     misc_mine[...] = misc
-    n_all[me] = normed
     misc_all[me] = misc
 
     grad_n = (grad_n * logit_scale).astype(BF16).astype(F32)
     along = jnp.mean(grad_n * x_wide, axis=-1, keepdims=True)
     grad_x = (inv_rms * grad_n - x_wide * (inv_rms * inv_rms * inv_rms * along)).astype(BF16)
+
+    to_peers(lambda target: misc_copy(target).start())
 
     def backward(k, grad_out):
         s = n_stage - 1 - k
@@ -267,30 +279,68 @@
 
         return result
 
-    to_peers(lambda target: n_copy(target).start())
     grad_in = lax.fori_loop(0, n_stage, backward, grad_x)
     dx_mine[...] = grad_in
-    to_peers(lambda target: misc_copy(target).start())
     dy_all[me] = dy_hist[me]
     dx_all[me] = grad_in
 
-    to_peers(lambda target: x_copy(target).wait_send())
-
-    def wait_from(buf, recv):
-        def one(k, carry):
-            source = lax.rem(me + k, n_stage)
-            pltpu.make_async_remote_copy(
-                src_ref=buf.at[source], dst_ref=buf.at[source], send_sem=dx_send.at[source], recv_sem=recv.at[source],
-                device_id=(dp, source), device_id_type=MESH).wait_recv()
-            return carry
-        lax.fori_loop(1, n_stage, one, 0)
-
-    wait_from(x_all, x_recv)
-    to_peers(lambda target: dx_copy(target).start())
-    wait_from(dy_all, dy_recv)
     wait_from(n_all, n_recv)
     wait_from(misc_all, misc_recv)
+    per_row = LANES // seq
+    for m in range(0, n_stage, per_row):
+        row = misc_all[m]
+        for k in range(1, per_row):
+            row = row + pltpu.roll(misc_all[m + k], k * seq, 1)
+        lse_row[:, pl.ds(m * seq, LANES)] = row
+    to_peers(lambda target: dx_copy(target).start())
+
+    half_rows = vocab // 2
+    rows, n_full, tail = chunks(half_rows, TABLE_ROWS)
+    count = n_stage * seq
+
+    def keep_copy(first, height, index):
+        return pltpu.make_async_copy(
+            head_part.at[pl.ds(first, height), :], head_hbm.at[pl.ds(core * half_rows + first, height), :], keep_sem.at[index])
+
+    def part_copy(first, height, index, owner):
+        return pltpu.make_async_remote_copy(
+            src_ref=head_part.at[pl.ds(first, height), :],
+            dst_ref=head_hbm.at[pl.ds(owner * half_rows + first, height), :],
+            send_sem=part_send.at[index], recv_sem=part_recv.at[index],
+            device_id=(dp, partner), device_id_type=MESH)
+
+    def pass_on(first, height, index):
+        keep_copy(first, height, index).start()
+        part_copy(first, height, index, core).start()
+
+    def head_rows(first, height):
+        every = n_all[...].reshape(count, dim)
+        tile = lax.div(core * half_rows + first, TILE)
+        z = (dot_nt(table[pl.ds(tile, height // TILE)].reshape(height, dim), every) * logit_scale).astype(BF16).astype(F32)
+        grad_z = jnp.exp(z - lse_row[0:1, :]).astype(BF16)
+        head_part[pl.ds(first, height), :] = dot_nn(grad_z, every) * logit_scale
+
+    def head_chunk(i, carry):
+        @pl.when(i > 0)
+        def _():
+            pass_on(pl.multiple_of((i - 1) * rows, TILE), rows, i - 1)
+
+        head_rows(pl.multiple_of(i * rows, rows), rows)
+        return carry
+
+    lax.fori_loop(0, n_full, head_chunk, 0)
+    if tail:
+        pass_on((n_full - 1) * rows, rows, n_full - 1)
+        head_rows(n_full * rows, tail)
+
+    to_peers(lambda target: x_copy(target).wait_send())
+    wait_from(x_all, x_recv)
+    wait_from(dy_all, dy_recv)
     wait_from(dx_all, dx_recv)
+    if tail:
+        pass_on(n_full * rows, tail, n_full)
+    else:
+        pass_on((n_full - 1) * rows, rows, n_full - 1)
     n_out[...] = n_all[...]
     misc_out[...] = misc_all[...]
     dx_out[...] = dx_all[...]
@@ -302,16 +352,74 @@
     for make in (dy_copy, n_copy, misc_copy, dx_copy):
         to_peers(lambda target, make=make: make(target).wait_send())
 
-
-def table_kernel(inv_count, tok_ref, lab_ref, misc_ref, n_ref, dx_ref, x_ref, dy_ref, up_ref, down_ref, table_hbm,
-                 out_hbm, loss_out, gup_out, gdown_out, table, acc, dx_wide, fix_rows, lse_row, table_sem, out_sem):
-    vocab, dim = table.shape
+    def finish(first, height, index):
+        keep_copy(first, height, index).wait()
+        part_copy(first, height, index, core).wait_send()
+        part_copy(first, height, index, 1 - core).wait_recv()
+
+    def finish_chunk(i, carry):
+        finish(pl.multiple_of(i * rows, rows), rows, i)
+        return carry
+
+    lax.fori_loop(0, n_full, finish_chunk, 0)
+    if tail:
+        finish(n_full * rows, tail, n_full)
+
+
+def table_kernel(inv_count, tok_ref, lab_ref, misc_ref, n_ref, dx_ref, x_ref, dy_ref, up_ref, down_ref, head_hbm,
+                 out_hbm, loss_out, gup_out, gdown_out, head, acc, acc_lab, dx_wide, fix_rows, head_sem, out_sem):
+    vocab, dim = acc.shape
     n_micro, seq, _ = n_ref.shape
-    count = n_micro * seq
     logit_scale = dim ** -0.5
-    table_copy = pltpu.make_async_copy(table_hbm, table, table_sem)
-    table_copy.start()
-    acc[...] = jnp.zeros_like(acc)
+    rows, n_full, tail = chunks(vocab, OUT_ROWS)
+
+    def head_copy(first, height, index):
+        return pltpu.make_async_copy(head_hbm.at[pl.ds(first, height), :], head.at[pl.ds(first, height), :], head_sem.at[index])
+
+    def out_copy(first, height, index):
+        return pltpu.make_async_copy(acc.at[pl.ds(first, height), :], out_hbm.at[pl.ds(first, height), :], out_sem.at[index])
+
+    def each(body):
+        def one(i, carry):
+            body(pl.multiple_of(i * rows, rows), rows, i)
+            return carry
+        lax.fori_loop(0, n_full, one, 0)
+        if tail:
+            body(n_full * rows, tail, n_full)
+
+    each(lambda *where: head_copy(*where).start())
+
+    def clear(first, height, index):
+        acc[pl.ds(first, height), :] = jnp.zeros((height, dim), F32)
+        acc_lab[pl.ds(first, height), :] = jnp.zeros((height, dim), F32)
+
+    each(clear)
+
+    eye = lax.broadcasted_iota(jnp.int32, (seq, LANES), 0) == lax.broadcasted_iota(jnp.int32, (seq, LANES), 1)
+    total = jnp.zeros((8, LANES), F32)
+    for m in range(n_micro):
+        misc = misc_ref[m]
+        total = total + misc
+        fix = jnp.sum(jnp.where(eye, misc[1:2, :], 0.0), axis=-1, keepdims=True) * logit_scale
+        fix_rows[pl.ds(m * seq, seq), :] = n_ref[m].astype(F32) * fix
+        dx_wide[pl.ds(m * seq, seq), :] = dx_ref[m].astype(F32)
+    loss_out[0] = jnp.max(total[2:3, :])
+
+    def scatter(m, carry):
+        for i in range(seq):
+            acc[pl.ds(tok_ref[m, i], 1), :] += dx_wide[pl.ds(m * seq + i, 1), :]
+            acc_lab[pl.ds(lab_ref[m, i], 1), :] += fix_rows[pl.ds(m * seq + i, 1), :]
+        return carry
+
+    lax.fori_loop(0, n_micro, scatter, 0)
+
+    def join(first, height, index):
+        head_copy(first, height, index).wait()
+        where = pl.ds(first, height)
+        acc[where, :] = head[where, :] + (acc[where, :] + acc_lab[where, :])
+        out_copy(first, height, index).start()
+
+    each(join)
 
     up, down = up_ref[0], down_ref[0]
     gup_out[...] = jnp.zeros_like(gup_out)
@@ -330,61 +438,7 @@
         return carry
 
     lax.fori_loop(0, n_micro // group, wgrad, 0)
-
-    eye = lax.broadcasted_iota(jnp.int32, (seq, LANES), 0) == lax.broadcasted_iota(jnp.int32, (seq, LANES), 1)
-    per_row = LANES // seq
-    total = jnp.zeros((8, LANES), F32)
-    for m in range(n_micro):
-        misc = misc_ref[m]
-        total = total + misc
-        fix = jnp.sum(jnp.where(eye, misc[1:2, :], 0.0), axis=-1, keepdims=True) * logit_scale
-        fix_rows[pl.ds(m * seq, seq), :] = n_ref[m].astype(F32) * fix
-        dx_wide[pl.ds(m * seq, seq), :] = dx_ref[m].astype(F32)
-        if m % per_row == 0:
-            row = misc
-            for k in range(1, per_row):
-                row = row + pltpu.roll(misc_ref[m + k], k * seq, 1)
-            lse_row[:, pl.ds(m * seq, LANES)] = row
-    loss_out[0] = jnp.max(total[2:3, :])
-
-    def scatter(m, carry):
-        def one(i, inner):
-            acc[pl.ds(tok_ref[m, i], 1), :] += dx_wide[pl.ds(m * seq + i, 1), :]
-            acc[pl.ds(lab_ref[m, i], 1), :] += fix_rows[pl.ds(m * seq + i, 1), :]
-            return inner
-        return lax.fori_loop(0, seq, one, carry, unroll=8)
-
-    lax.fori_loop(0, n_micro, scatter, 0)
-    table_copy.wait()
-
-    rows, n_full, tail = chunks(vocab, TABLE_ROWS)
-    lse = lse_row[0:1, :]
-
-    def out_copy(first, height, index):
-        return pltpu.make_async_copy(acc.at[pl.ds(first, height), :], out_hbm.at[pl.ds(first, height), :], out_sem.at[index])
-
-    def part(first, height, index):
-        normed = n_ref[...].reshape(count, dim)
-        z = (dot_nt(table[pl.ds(first, height), :], normed) * logit_scale).astype(BF16).astype(F32)
-        grad_z = jnp.exp(z - lse).astype(BF16)
-        acc[pl.ds(first, height), :] += dot_nn(grad_z, normed) * logit_scale
-        out_copy(first, height, index).start()
-
-    def loop(i, carry):
-        part(pl.multiple_of(i * rows, rows), rows, i)
-        return carry
-
-    lax.fori_loop(0, n_full, loop, 0)
-    if tail:
-        part(n_full * rows, tail, n_full)
-
-    def drain(i, carry):
-        out_copy(pl.multiple_of(i * rows, rows), rows, i).wait()
-        return carry
-
-    lax.fori_loop(0, n_full, drain, 0)
-    if tail:
-        out_copy(n_full * rows, tail, n_full).wait()
+    each(lambda *where: out_copy(*where).wait())
 
 
 def solution(mesh):
@@ -401,13 +455,14 @@
         hbm = pl.BlockSpec(memory_space=pl.ANY)
         dma = pltpu.SemaphoreType.DMA
 
+        n_parts = -(-vocab // (2 * TABLE_ROWS))
         act = jax.ShapeDtypeStruct((n_stage, seq, dim), BF16)
-        n_all, dx_all, x_all, dy_all, misc = pl.pallas_call(
+        n_all, dx_all, x_all, dy_all, misc, head = pl.pallas_call(
             functools.partial(step_kernel, n_stage, inv_count),
             name="step",
-            out_shape=(act, act, act, act, jax.ShapeDtypeStruct((n_stage, 8, LANES), F32)),
+            out_shape=(act, act, act, act, jax.ShapeDtypeStruct((n_stage, 8, LANES), F32), jax.ShapeDtypeStruct((vocab, dim), F32)),
             in_specs=[smem, vmem, hbm, vmem, vmem],
-            out_specs=(vmem,) * 5,
+            out_specs=(vmem,) * 5 + (hbm,),
             scratch_shapes=[
                 pltpu.VMEM((vocab // TILE, TILE, dim), BF16),
                 pltpu.VMEM((n_stage, dim, ffn), BF16),
@@ -420,6 +475,8 @@
                 pltpu.VMEM((8, LANES), F32),
                 pltpu.VMEM((seq, dim), BF16),
                 pltpu.VMEM((seq, dim), F32),
+                pltpu.VMEM((8, count), F32),
+                pltpu.VMEM((vocab // 2, dim), F32),
                 pltpu.VMEM((n_stage, seq, dim), BF16),
                 pltpu.VMEM((n_stage, 8, LANES), F32),
                 pltpu.VMEM((n_stage, seq, dim), BF16),
@@ -428,11 +485,12 @@
                 dma, dma((n_stage,)), dma((n_stage,)), dma((3, n_stage)), dma((3, n_stage)),
                 dma((n_stage,)), dma((n_stage,)), dma((n_stage,)), dma((n_stage,)), dma((n_stage,)),
                 dma((n_stage,)), dma((n_stage,)), dma((n_stage,)), dma((n_stage,)), dma((n_stage,)),
+                dma((n_parts,)), dma((n_parts,)), dma((n_parts,)),
             ],
             compiler_params=pltpu.CompilerParams(collective_id=0, has_side_effects=True),
         )(tokens, labels, emb_table.reshape(vocab // TILE, TILE, dim), w_up, w_down)
 
-        n_parts = -(-vocab // TABLE_ROWS)
+        n_outs = -(-vocab // OUT_ROWS)
         grad_emb, loss, g_up, g_down = pl.pallas_call(
             functools.partial(table_kernel, inv_count),
             name="table_grad",
@@ -445,14 +503,14 @@
             in_specs=[smem, smem, vmem, vmem, vmem, vmem, vmem, vmem, vmem, hbm],
             out_specs=(hbm, smem, vmem, vmem),
             scratch_shapes=[
-                pltpu.VMEM((vocab, dim), BF16),
+                pltpu.VMEM((vocab, dim), F32),
+                pltpu.VMEM((vocab, dim), F32),
                 pltpu.VMEM((vocab, dim), F32),
                 pltpu.VMEM((count, dim), F32),
                 pltpu.VMEM((count, dim), F32),
-                pltpu.VMEM((8, count), F32),
-                dma, dma((n_parts,)),
+                dma((n_outs,)), dma((n_outs,)),
             ],
-        )(tokens, labels, misc, n_all, dx_all, x_all, dy_all, w_up, w_down, emb_table)
+        )(tokens, labels, misc, n_all, dx_all, x_all, dy_all, w_up, w_down, head)
         return loss, g_up[None], g_down[None], grad_emb
 
     return jax.shard_map(device_fn, mesh=mesh, in_specs=(P("dp", None), P("dp", None), P(None, None), P("stage", None, None), P("stage", None, None)), out_specs=(P("dp"), P(("dp", "stage"), None, None), P(("dp", "stage"), None, None), P("dp", None)), check_vma=False)

time: 136 us -> 104 us (0.76)
  Pallas kernels: 135 us -> 103 us
    pallas_call x1, Pallas kernels: 53.4 us -> 15.6 us  [device_fn(): pl.pallas_call(functools.partial(table_kernel, inv_count), name='table_gr...]
    pallas_call x1, Pallas kernels: 81.9 us -> 87.7 us  [device_fn(): pl.pallas_call(functools.partial(step_kernel, n_stage, inv_count), name='...]
where the time goes in v3:
time: 104 us
  Pallas kernels  103 us (99%)
    pallas_call x1, Pallas kernels, device_fn(): pl.pallas_call(functools.partial(step_kernel, n_stage, inv_count), name='...  87.7 us
    pallas_call x1, Pallas kernels, device_fn(): pl.pallas_call(functools.partial(table_kernel, inv_count), name='table_gr...  15.6 us

profile of v3, /device:TPU:21, one launch (start us, length us, event | category | flops | bytes accessed | tf_op | source)
XLA Modules:
  0.0 103.9 jit_solution(350041299715578705)
XLA Ops:
  0.6 87.7 %step.1 = (bf16[16,64,128]{2,1,0:T(8,128)(2,1)}, bf16[16,64,128]{2,1,0:T(8,128)(2,1)}, bf16[16,64,128]{2,1,0:T(8,128)(2,1)}, bf16[16,64,128]{2,1,0:T(8,128)(2,1)...) custom-call(s32[16,64]{1,0:T(8,128)} %tok_ref.3, s32[16,64]{1,0:T(8,128)} %lab_ref.3, bf16[1912,16,128]{2,1,0:T(8,128)(2,1)} %bitcast.3, ...), custom_call_target="tpu_custom_call" | custom-call | tf_op jit(solution)/shard_map/step/pallas_call | solution.py:460
  88.3 15.6 %table_grad.1 = (f32[30592,128]{1,0:T(8,128)}, f32[1]{0:T(128)}, f32[128,512]{1,0:T(8,128)}, f32[512,128]{1,0:T(8,128)}) custom-call(s32[16,64]{1,0:T(8,128)} %tok_ref.3, s32[16,64]{1,0:T(8,128)} %lab_ref.3, f32[16,8,128]{2,1,0:T(8,128)} %get-tuple-element.14.misc_ref, bf16[16,64,128]{2,1,0:T(8,128)(2,1)} %get-tuple-element.15.n_ref, ...), custom_call_target="tpu_custom_call" | custom-call | tf_op jit(solution)/shard_map/table_grad/pallas_call | solution.py:494

commit v4 on v3

--- a/solution.py
+++ b/solution.py
@@ -13,7 +13,7 @@
 MESH = pl.DeviceIdType.MESH
 LANES = 128
 TILE = 16
-HEAD_COLS = 1024
+HEAD_COLS = 4096
 TABLE_ROWS = 2048
 OUT_ROWS = 2048
 GELU_C = math.sqrt(2.0 / math.pi)
@@ -47,11 +47,11 @@
     return size, total // size, total % size
 
 
-def step_kernel(n_stage, inv_count, tok_ref, lab_ref, table_hbm, w_up_ref, w_down_ref,
+def step_kernel(n_stage, inv_count, tok_hbm, lab_hbm, table_hbm, w_up_hbm, w_down_hbm,
                 n_out, dx_out, x_out, dy_out, misc_out, head_hbm,
-                table, up_all, down_all, x_hist, pre_hist, dy_hist, logits,
+                tok_ref, lab_ref, table, up_all, down_all, x_hist, pre_hist, dy_hist, logits,
                 n_mine, misc_mine, dx_mine, x_rows, lse_row, head_part, n_all, misc_all, dx_all, x_all, dy_all,
-                table_sem, up_recv, down_recv, up_send, down_send,
+                in_sem, out_sem, table_sem, up_recv, down_recv, up_send, down_send,
                 x_recv, dy_recv, n_recv, misc_recv, dx_recv,
                 x_send, dy_send, n_send, misc_send, dx_send, keep_sem, part_send, part_recv):
     me = lax.axis_index("stage")
@@ -69,6 +69,14 @@
 
     right, left, partner = slot_at(1, core), slot_at(-1, core), chip * 2 + (1 - core)
 
+    loads = [
+        pltpu.make_async_copy(w_up_hbm.at[0], up_all.at[me], in_sem.at[0]),
+        pltpu.make_async_copy(w_down_hbm.at[0], down_all.at[me], in_sem.at[1]),
+        pltpu.make_async_copy(tok_hbm, tok_ref, in_sem.at[2]),
+        pltpu.make_async_copy(lab_hbm, lab_ref, in_sem.at[3]),
+    ]
+    for load in loads:
+        load.start()
     table_copy = pltpu.make_async_copy(table_hbm, table, table_sem)
     table_copy.start()
 
@@ -80,16 +88,18 @@
 
     lax.fori_loop(1, n_stage, greet, 0)
     pl.semaphore_wait(barrier, n_stage - 1)
-
-    def up_copy(slot, way, target, own=False):
+    for load in loads:
+        load.wait()
+
+    def up_copy(slot, way, target):
         return pltpu.make_async_remote_copy(
-            src_ref=w_up_ref.at[0] if own else up_all.at[slot], dst_ref=up_all.at[slot],
+            src_ref=up_all.at[slot], dst_ref=up_all.at[slot],
             send_sem=up_send.at[way, slot], recv_sem=up_recv.at[slot],
             device_id=(dp, target), device_id_type=MESH)
 
-    def down_copy(slot, way, target, own=False):
+    def down_copy(slot, way, target):
         return pltpu.make_async_remote_copy(
-            src_ref=w_down_ref.at[0] if own else down_all.at[slot], dst_ref=down_all.at[slot],
+            src_ref=down_all.at[slot], dst_ref=down_all.at[slot],
             send_sem=down_send.at[way, slot], recv_sem=down_recv.at[slot],
             device_id=(dp, target), device_id_type=MESH)
 
@@ -100,10 +110,8 @@
         sends.append(copy)
 
     for way, target in ((0, right), (1, left), (2, partner)):
-        send(up_copy(me, way, target, own=True))
-        send(down_copy(me, way, target, own=True))
-    up_all[me] = w_up_ref[0]
-    down_all[me] = w_down_ref[0]
+        send(up_copy(me, way, target))
+        send(down_copy(me, way, target))
 
     table_copy.wait()
     row_iota = lax.broadcasted_iota(jnp.int32, (TILE, dim), 0)
@@ -293,6 +301,10 @@
             row = row + pltpu.roll(misc_all[m + k], k * seq, 1)
         lse_row[:, pl.ds(m * seq, LANES)] = row
     to_peers(lambda target: dx_copy(target).start())
+    results = [pltpu.make_async_copy(src, dst, out_sem.at[i]) for i, (src, dst) in enumerate(
+        ((n_all, n_out), (misc_all, misc_out), (x_all, x_out), (dy_all, dy_out), (dx_all, dx_out)))]
+    results[0].start()
+    results[1].start()
 
     half_rows = vocab // 2
     rows, n_full, tail = chunks(half_rows, TABLE_ROWS)
@@ -329,28 +341,23 @@
         return carry
 
     lax.fori_loop(0, n_full, head_chunk, 0)
-    if tail:
-        pass_on((n_full - 1) * rows, rows, n_full - 1)
-        head_rows(n_full * rows, tail)
-
-    to_peers(lambda target: x_copy(target).wait_send())
+    pass_on((n_full - 1) * rows, rows, n_full - 1)
     wait_from(x_all, x_recv)
     wait_from(dy_all, dy_recv)
     wait_from(dx_all, dx_recv)
+    for result in results[2:]:
+        result.start()
+    if tail:
+        head_rows(n_full * rows, tail)
+    to_peers(lambda target: x_copy(target).wait_send())
+    for copy in sends:
+        copy.wait_send()
     if tail:
         pass_on(n_full * rows, tail, n_full)
-    else:
-        pass_on((n_full - 1) * rows, rows, n_full - 1)
-    n_out[...] = n_all[...]
-    misc_out[...] = misc_all[...]
-    dx_out[...] = dx_all[...]
-    x_out[...] = x_all[...]
-    dy_out[...] = dy_all[...]
-
-    for copy in sends:
-        copy.wait_send()
     for make in (dy_copy, n_copy, misc_copy, dx_copy):
         to_peers(lambda target, make=make: make(target).wait_send())
+    for result in results:
+        result.wait()
 
     def finish(first, height, index):
         keep_copy(first, height, index).wait()
@@ -366,8 +373,10 @@
         finish(n_full * rows, tail, n_full)
 
 
-def table_kernel(inv_count, tok_ref, lab_ref, misc_ref, n_ref, dx_ref, x_ref, dy_ref, up_ref, down_ref, head_hbm,
-                 out_hbm, loss_out, gup_out, gdown_out, head, acc, acc_lab, dx_wide, fix_rows, head_sem, out_sem):
+def table_kernel(tok_hbm, lab_hbm, misc_hbm, n_hbm, dx_hbm, x_hbm, dy_hbm, up_hbm, down_hbm, head_hbm,
+                 out_hbm, loss_out, gup_hbm, gdown_hbm,
+                 tok_ref, lab_ref, misc_ref, n_ref, dx_ref, x_ref, dy_ref, up_ref, down_ref, gup_out, gdown_out,
+                 head, acc, acc_lab, dx_wide, fix_rows, in_sem, grad_sem, head_sem, out_sem):
     vocab, dim = acc.shape
     n_micro, seq, _ = n_ref.shape
     logit_scale = dim ** -0.5
@@ -387,13 +396,22 @@
         if tail:
             body(n_full * rows, tail, n_full)
 
+    loads = [pltpu.make_async_copy(src, dst, in_sem.at[i]) for i, (src, dst) in enumerate((
+        (tok_hbm, tok_ref), (lab_hbm, lab_ref), (misc_hbm, misc_ref), (n_hbm, n_ref), (dx_hbm, dx_ref),
+        (x_hbm, x_ref), (dy_hbm, dy_ref), (up_hbm.at[0], up_ref), (down_hbm.at[0], down_ref)))]
+    for load in loads[:5]:
+        load.start()
     each(lambda *where: head_copy(*where).start())
+    for load in loads[5:]:
+        load.start()
 
     def clear(first, height, index):
         acc[pl.ds(first, height), :] = jnp.zeros((height, dim), F32)
         acc_lab[pl.ds(first, height), :] = jnp.zeros((height, dim), F32)
 
     each(clear)
+    for load in loads[:5]:
+        load.wait()
 
     eye = lax.broadcasted_iota(jnp.int32, (seq, LANES), 0) == lax.broadcasted_iota(jnp.int32, (seq, LANES), 1)
     total = jnp.zeros((8, LANES), F32)
@@ -421,7 +439,9 @@
 
     each(join)
 
-    up, down = up_ref[0], down_ref[0]
+    for load in loads[5:]:
+        load.wait()
+    up, down = up_ref[...], down_ref[...]
     gup_out[...] = jnp.zeros_like(gup_out)
     gdown_out[...] = jnp.zeros_like(gdown_out)
     group = max(1, 256 // seq)
@@ -438,6 +458,11 @@
         return carry
 
     lax.fori_loop(0, n_micro // group, wgrad, 0)
+    grads = [pltpu.make_async_copy(gup_out, gup_hbm, grad_sem.at[0]), pltpu.make_async_copy(gdown_out, gdown_hbm, grad_sem.at[1])]
+    for grad in grads:
+        grad.start()
+    for grad in grads:
+        grad.wait()
     each(lambda *where: out_copy(*where).wait())
 
 
@@ -461,9 +486,11 @@
             functools.partial(step_kernel, n_stage, inv_count),
             name="step",
             out_shape=(act, act, act, act, jax.ShapeDtypeStruct((n_stage, 8, LANES), F32), jax.ShapeDtypeStruct((vocab, dim), F32)),
-            in_specs=[smem, vmem, hbm, vmem, vmem],
-            out_specs=(vmem,) * 5 + (hbm,),
+            in_specs=[hbm] * 5,
+            out_specs=(hbm,) * 6,
             scratch_shapes=[
+                pltpu.SMEM((n_micro, seq), jnp.int32),
+                pltpu.VMEM((n_micro, seq), jnp.int32),
                 pltpu.VMEM((vocab // TILE, TILE, dim), BF16),
                 pltpu.VMEM((n_stage, dim, ffn), BF16),
                 pltpu.VMEM((n_stage, ffn, dim), BF16),
@@ -482,7 +509,7 @@
                 pltpu.VMEM((n_stage, seq, dim), BF16),
                 pltpu.VMEM((n_stage, seq, dim), BF16),
                 pltpu.VMEM((n_stage, seq, dim), BF16),
-                dma, dma((n_stage,)), dma((n_stage,)), dma((3, n_stage)), dma((3, n_stage)),
+                dma((4,)), dma((5,)), dma, dma((n_stage,)), dma((n_stage,)), dma((3, n_stage)), dma((3, n_stage)),
                 dma((n_stage,)), dma((n_stage,)), dma((n_stage,)), dma((n_stage,)), dma((n_stage,)),
                 dma((n_stage,)), dma((n_stage,)), dma((n_stage,)), dma((n_stage,)), dma((n_stage,)),
                 dma((n_parts,)), dma((n_parts,)), dma((n_parts,)),
@@ -492,7 +519,7 @@
 
         n_outs = -(-vocab // OUT_ROWS)
         grad_emb, loss, g_up, g_down = pl.pallas_call(
-            functools.partial(table_kernel, inv_count),
+            table_kernel,
             name="table_grad",
             out_shape=(
                 jax.ShapeDtypeStruct((vocab, dim), F32),
@@ -500,15 +527,26 @@
                 jax.ShapeDtypeStruct((dim, ffn), F32),
                 jax.ShapeDtypeStruct((ffn, dim), F32),
             ),
-            in_specs=[smem, smem, vmem, vmem, vmem, vmem, vmem, vmem, vmem, hbm],
-            out_specs=(hbm, smem, vmem, vmem),
+            in_specs=[hbm] * 10,
+            out_specs=(hbm, smem, hbm, hbm),
             scratch_shapes=[
+                pltpu.SMEM((n_micro, seq), jnp.int32),
+                pltpu.SMEM((n_micro, seq), jnp.int32),
+                pltpu.VMEM((n_stage, 8, LANES), F32),
+                pltpu.VMEM((n_stage, seq, dim), BF16),
+                pltpu.VMEM((n_stage, seq, dim), BF16),
+                pltpu.VMEM((n_stage, seq, dim), BF16),
+                pltpu.VMEM((n_stage, seq, dim), BF16),
+                pltpu.VMEM((dim, ffn), BF16),
+                pltpu.VMEM((ffn, dim), BF16),
+                pltpu.VMEM((dim, ffn), F32),
+                pltpu.VMEM((ffn, dim), F32),
                 pltpu.VMEM((vocab, dim), F32),
                 pltpu.VMEM((vocab, dim), F32),
                 pltpu.VMEM((vocab, dim), F32),
                 pltpu.VMEM((count, dim), F32),
                 pltpu.VMEM((count, dim), F32),
-                dma((n_outs,)), dma((n_outs,)),
+                dma((9,)), dma((2,)), dma((n_outs,)), dma((n_outs,)),
             ],
         )(tokens, labels, misc, n_all, dx_all, x_all, dy_all, w_up, w_down, head)
         return loss, g_up[None], g_down[None], grad_emb

time: 104 us -> 95.3 us (0.916)
  Pallas kernels: 103 us -> 94.3 us
    pallas_call x1, Pallas kernels: 87.7 us -> 79.8 us  [device_fn(): pl.pallas_call(functools.partial(step_kernel, n_stage, inv_count), name='...]
    pallas_call x1, Pallas kernels: 15.6 us -> 14.4 us  [device_fn(): pl.pallas_call(table_kernel, name='table_grad', out_shape=(jax.ShapeDtype...]
where the time goes in v4:
time: 95.3 us; the launch traced here: 94.9 us
  Pallas kernels  94.3 us (99%)
    pallas_call x1, Pallas kernels, device_fn(): pl.pallas_call(functools.partial(step_kernel, n_stage, inv_count), name='...  79.8 us
    pallas_call x1, Pallas kernels, device_fn(): pl.pallas_call(table_kernel, name='table_grad', out_shape=(jax.ShapeDtype...  14.4 us

profile of v4, /device:TPU:21, one launch (start us, length us, event | category | flops | bytes accessed | tf_op | source)
XLA Modules:
  0.0 94.9 jit_solution(416060733459950108)
XLA Ops:
  0.6 79.8 %step.1 = (bf16[16,64,128]{2,1,0:T(8,128)(2,1)}, bf16[16,64,128]{2,1,0:T(8,128)(2,1)}, bf16[16,64,128]{2,1,0:T(8,128)(2,1)}, bf16[16,64,128]{2,1,0:T(8,128)(2,1)...) custom-call(s32[16,64]{1,0:T(8,128)} %tok_hbm.3, s32[16,64]{1,0:T(8,128)} %lab_hbm.3, bf16[1912,16,128]{2,1,0:T(8,128)(2,1)} %bitcast.3, ...), custom_call_target="tpu_custom_call" | custom-call | tf_op jit(solution)/shard_map/step/pallas_call | solution.py:485
  80.5 14.4 %table_grad.1 = (f32[30592,128]{1,0:T(8,128)}, f32[1]{0:T(128)}, f32[128,512]{1,0:T(8,128)}, f32[512,128]{1,0:T(8,128)}) custom-call(s32[16,64]{1,0:T(8,128)} %tok_hbm.3, s32[16,64]{1,0:T(8,128)} %lab_hbm.3, f32[16,8,128]{2,1,0:T(8,128)} %get-tuple-element.14.misc_hbm, bf16[16,64,128]{2,1,0:T(8,128)(2,1)} %get-tuple-element.15.n_hbm, ...), custom_call_target="tpu_custom_call" | custom-call | tf_op jit(solution)/shard_map/table_grad/pallas_call | solution.py:521

commit v5 on v4

--- a/solution.py
+++ b/solution.py
@@ -47,11 +47,11 @@
     return size, total // size, total % size
 
 
-def step_kernel(n_stage, inv_count, tok_hbm, lab_hbm, table_hbm, w_up_hbm, w_down_hbm,
+def step_kernel(n_stage, n_dp, inv_count, tok_hbm, lab_hbm, table_hbm, w_up_hbm, w_down_hbm,
                 n_out, dx_out, x_out, dy_out, misc_out, head_hbm,
                 tok_ref, lab_ref, table, up_all, down_all, x_hist, pre_hist, dy_hist, logits,
                 n_mine, misc_mine, dx_mine, x_rows, lse_row, head_part, n_all, misc_all, dx_all, x_all, dy_all,
-                in_sem, out_sem, table_sem, up_recv, down_recv, up_send, down_send,
+                in_sem, out_sem, table_sem, up_recv, down_recv, up_send, down_send, side_recv, side_send,
                 x_recv, dy_recv, n_recv, misc_recv, dx_recv,
                 x_send, dy_send, n_send, misc_send, dx_send, keep_sem, part_send, part_recv):
     me = lax.axis_index("stage")
@@ -87,21 +87,53 @@
         return carry
 
     lax.fori_loop(1, n_stage, greet, 0)
-    pl.semaphore_wait(barrier, n_stage - 1)
+    paired = n_dp % 2 == 0
+    side = dp + 1 - 2 * lax.rem(dp, 2)
+    if paired:
+        pl.semaphore_signal(barrier, inc=1, device_id=(side, me), device_id_type=MESH)
+    pl.semaphore_wait(barrier, n_stage if paired else n_stage - 1)
     for load in loads:
         load.wait()
 
-    def up_copy(slot, way, target):
+    parity = lax.rem(dp, 2)
+    up_rows, down_rows = up_all.shape[1], down_all.shape[1]
+
+    def up_part(kind):
+        left_out = up_rows // 64 * 16
+        if kind == "whole" or not paired:
+            return pl.ds(0, up_rows)
+        if kind == "ring":
+            return pl.ds(pl.multiple_of(parity * left_out, 16), up_rows - left_out)
+        mine = parity if kind == "give" else 1 - parity
+        return pl.ds(pl.multiple_of(mine * (up_rows - left_out), 16), left_out)
+
+    def down_part(kind):
+        left_out = down_rows * 5 // 256 * 16
+        if kind == "whole" or not paired:
+            return pl.ds(0, down_rows)
+        if kind == "ring":
+            return pl.ds(pl.multiple_of(parity * left_out, 16), down_rows - left_out)
+        mine = parity if kind == "give" else 1 - parity
+        return pl.ds(pl.multiple_of(mine * (down_rows - left_out), 16), left_out)
+
+    def up_copy(slot, way, target, kind):
+        ref = up_all.at[slot, up_part(kind)]
         return pltpu.make_async_remote_copy(
-            src_ref=up_all.at[slot], dst_ref=up_all.at[slot],
-            send_sem=up_send.at[way, slot], recv_sem=up_recv.at[slot],
+            src_ref=ref, dst_ref=ref, send_sem=up_send.at[way, slot], recv_sem=up_recv.at[slot],
             device_id=(dp, target), device_id_type=MESH)
 
-    def down_copy(slot, way, target):
+    def down_copy(slot, way, target, kind):
+        ref = down_all.at[slot, down_part(kind)]
         return pltpu.make_async_remote_copy(
-            src_ref=down_all.at[slot], dst_ref=down_all.at[slot],
-            send_sem=down_send.at[way, slot], recv_sem=down_recv.at[slot],
+            src_ref=ref, dst_ref=ref, send_sem=down_send.at[way, slot], recv_sem=down_recv.at[slot],
             device_id=(dp, target), device_id_type=MESH)
+
+    def side_copy(which, slot, kind):
+        ref = up_all.at[slot, up_part(kind)] if which == 0 else down_all.at[slot, down_part(kind)]
+        give = kind == "give"
+        return pltpu.make_async_remote_copy(
+            src_ref=ref, dst_ref=ref, send_sem=side_send.at[0 if give else 1, which, slot], recv_sem=side_recv.at[which, slot],
+            device_id=(side, me) if give else (dp, partner), device_id_type=MESH)
 
     sends = []
 
@@ -109,9 +141,9 @@
         copy.start()
         sends.append(copy)
 
-    for way, target in ((0, right), (1, left), (2, partner)):
-        send(up_copy(me, way, target))
-        send(down_copy(me, way, target))
+    for way, target, kind in ((0, right, "ring"), (1, left, "ring"), (2, partner, "whole")):
+        send(up_copy(me, way, target, kind))
+        send(down_copy(me, way, target, kind))
 
     table_copy.wait()
     row_iota = lax.broadcasted_iota(jnp.int32, (TILE, dim), 0)
@@ -126,30 +158,43 @@
     lax.fori_loop(0, seq, embed, 0)
     x_now = x_rows[...].astype(BF16)
 
+    def arrived(copy, which, slot, forward):
+        copy.wait_recv()
+        if forward is not None:
+            send(forward)
+        if paired:
+            send(side_copy(which, slot, "give"))
+
     for t in range(1, half + 1):
         slot_l, slot_r = slot_at(-t, core), slot_at(t, core)
-        up_copy(slot_l, 0, right).wait_recv()
-        if t < half:
-            send(up_copy(slot_l, 0, right))
-        send(up_copy(slot_l, 2, partner))
-        down_copy(slot_r, 1, left).wait_recv()
-        if t < half:
-            send(down_copy(slot_r, 1, left))
-        send(down_copy(slot_r, 2, partner))
-        if t < half:
-            down_copy(slot_l, 0, right).wait_recv()
-            if t < half - 1:
-                send(down_copy(slot_l, 0, right))
-            send(down_copy(slot_l, 2, partner))
-            up_copy(slot_r, 1, left).wait_recv()
-            if t < half - 1:
-                send(up_copy(slot_r, 1, left))
-            send(up_copy(slot_r, 2, partner))
+        whole, onward = t < half, t < half - 1
+        up_l, down_r = up_copy(slot_l, 0, right, "ring"), down_copy(slot_r, 1, left, "ring")
+        arrived(up_l, 0, slot_l, up_l if whole else None)
+        arrived(down_r, 1, slot_r, down_r if whole else None)
+        if whole:
+            down_l, up_r = down_copy(slot_l, 0, right, "ring"), up_copy(slot_r, 1, left, "ring")
+            arrived(down_l, 1, slot_l, down_l if onward else None)
+            arrived(up_r, 0, slot_r, up_r if onward else None)
+            send(down_copy(slot_l, 2, partner, "ring"))
+            send(up_copy(slot_r, 2, partner, "ring"))
+        send(up_copy(slot_l, 2, partner, "ring"))
+        send(down_copy(slot_r, 2, partner, "ring"))
+
+    if paired:
+        for t in [d for k in range(1, half) for d in (-k, k)] + [half]:
+            for which in (0, 1):
+                taken = side_copy(which, slot_at(t, core), "take")
+                taken.wait_recv()
+                send(taken)
 
     for t in range(n_chip):
         slot = slot_at(t, 1 - core)
-        up_copy(slot, 2, partner).wait_recv()
-        down_copy(slot, 2, partner).wait_recv()
+        kind = "whole" if t == 0 else "ring"
+        up_copy(slot, 2, partner, kind).wait_recv()
+        down_copy(slot, 2, partner, kind).wait_recv()
+        if paired and t > 0:
+            side_copy(0, slot, "take").wait_recv()
+            side_copy(1, slot, "take").wait_recv()
 
     def forward(s, x_act):
         x_hist[s] = x_act
@@ -483,7 +528,7 @@
         n_parts = -(-vocab // (2 * TABLE_ROWS))
         act = jax.ShapeDtypeStruct((n_stage, seq, dim), BF16)
         n_all, dx_all, x_all, dy_all, misc, head = pl.pallas_call(
-            functools.partial(step_kernel, n_stage, inv_count),
+            functools.partial(step_kernel, n_stage, mesh.shape["dp"], inv_count),
             name="step",
             out_shape=(act, act, act, act, jax.ShapeDtypeStruct((n_stage, 8, LANES), F32), jax.ShapeDtypeStruct((vocab, dim), F32)),
             in_specs=[hbm] * 5,
@@ -510,6 +555,7 @@
                 pltpu.VMEM((n_stage, seq, dim), BF16),
                 pltpu.VMEM((n_stage, seq, dim), BF16),
                 dma((4,)), dma((5,)), dma, dma((n_stage,)), dma((n_stage,)), dma((3, n_stage)), dma((3, n_stage)),
+                dma((2, n_stage)), dma((2, 2, n_stage)),
                 dma((n_stage,)), dma((n_stage,)), dma((n_stage,)), dma((n_stage,)), dma((n_stage,)),
                 dma((n_stage,)), dma((n_stage,)), dma((n_stage,)), dma((n_stage,)), dma((n_stage,)),
                 dma((n_parts,)), dma((n_parts,)), dma((n_parts,)),

time: 95.3 us -> 95.8 us (level)
  no operation moved by 1% of the time
where the time goes in v5:
time: 95.8 us; the launch traced here: 95.7 us
  Pallas kernels  95.1 us (99%)
    pallas_call x1, Pallas kernels, device_fn(): pl.pallas_call(functools.partial(step_kernel, n_stage, mesh.shape['dp'],...  80.6 us
    pallas_call x1, Pallas kernels, device_fn(): pl.pallas_call(table_kernel, name='table_grad', out_shape=(jax.ShapeDtype...  14.4 us

profile of v5, /device:TPU:21, one launch (start us, length us, event | category | flops | bytes accessed | tf_op | source)
XLA Modules:
  0.0 95.7 jit_solution(12898104453969076786)
XLA Ops:
  0.6 80.6 %step.1 = (bf16[16,64,128]{2,1,0:T(8,128)(2,1)}, bf16[16,64,128]{2,1,0:T(8,128)(2,1)}, bf16[16,64,128]{2,1,0:T(8,128)(2,1)}, bf16[16,64,128]{2,1,0:T(8,128)(2,1)...) custom-call(s32[16,64]{1,0:T(8,128)} %tok_hbm.3, s32[16,64]{1,0:T(8,128)} %lab_hbm.3, bf16[1912,16,128]{2,1,0:T(8,128)(2,1)} %bitcast.3, ...), custom_call_target="tpu_custom_call" | custom-call | tf_op jit(solution)/shard_map/step/pallas_call | solution.py:530
  81.3 14.4 %table_grad.1 = (f32[30592,128]{1,0:T(8,128)}, f32[1]{0:T(128)}, f32[128,512]{1,0:T(8,128)}, f32[512,128]{1,0:T(8,128)}) custom-call(s32[16,64]{1,0:T(8,128)} %tok_hbm.3, s32[16,64]{1,0:T(8,128)} %lab_hbm.3, f32[16,8,128]{2,1,0:T(8,128)} %get-tuple-element.14.misc_hbm, bf16[16,64,128]{2,1,0:T(8,128)(2,1)} %get-tuple-element.15.n_hbm, ...), custom_call_target="tpu_custom_call" | custom-call | tf_op jit(solution)/shard_map/table_grad/pallas_call | solution.py:567

commit v6 on v5

--- a/solution.py
+++ b/solution.py
@@ -82,16 +82,12 @@
 
     barrier = pltpu.get_barrier_semaphore()
 
-    def greet(k, carry):
-        pl.semaphore_signal(barrier, inc=1, device_id=(dp, lax.rem(me + k, n_stage)), device_id_type=MESH)
-        return carry
-
-    lax.fori_loop(1, n_stage, greet, 0)
     paired = n_dp % 2 == 0
     side = dp + 1 - 2 * lax.rem(dp, 2)
-    if paired:
-        pl.semaphore_signal(barrier, inc=1, device_id=(side, me), device_id_type=MESH)
-    pl.semaphore_wait(barrier, n_stage if paired else n_stage - 1)
+    greeted = [(dp, right), (dp, left), (dp, partner)] + ([(side, me)] if paired else [])
+    for peer in greeted:
+        pl.semaphore_signal(barrier, inc=1, device_id=peer, device_id_type=MESH)
+    pl.semaphore_wait(barrier, len(greeted))
     for load in loads:
         load.wait()
 
@@ -142,8 +138,8 @@
         sends.append(copy)
 
     for way, target, kind in ((0, right, "ring"), (1, left, "ring"), (2, partner, "whole")):
-        send(up_copy(me, way, target, kind))
-        send(down_copy(me, way, target, kind))
+        for copy in (down_copy, up_copy) if way == 1 else (up_copy, down_copy):
+            send(copy(me, way, target, kind))
 
     table_copy.wait()
     row_iota = lax.broadcasted_iota(jnp.int32, (TILE, dim), 0)

time: 95.8 us -> 94 us (0.981)
  Pallas kernels: 95.1 us -> 93.2 us
    pallas_call x1, Pallas kernels: 80.6 us -> 78.8 us  [device_fn(): pl.pallas_call(functools.partial(step_kernel, n_stage, mesh.shape['dp'],...]
where the time goes in v6:
time: 94 us; the launch traced here: 93.9 us
  Pallas kernels  93.2 us (99%)
    pallas_call x1, Pallas kernels, device_fn(): pl.pallas_call(functools.partial(step_kernel, n_stage, mesh.shape['dp'],...  78.8 us
    pallas_call x1, Pallas kernels, device_fn(): pl.pallas_call(table_kernel, name='table_grad', out_shape=(jax.ShapeDtype...  14.4 us

profile of v6, /device:TPU:21, one launch (start us, length us, event | category | flops | bytes accessed | tf_op | source)
XLA Modules:
  0.0 93.9 jit_solution(7415822621465211633)
XLA Ops:
  0.6 78.8 %step.1 = (bf16[16,64,128]{2,1,0:T(8,128)(2,1)}, bf16[16,64,128]{2,1,0:T(8,128)(2,1)}, bf16[16,64,128]{2,1,0:T(8,128)(2,1)}, bf16[16,64,128]{2,1,0:T(8,128)(2,1)...) custom-call(s32[16,64]{1,0:T(8,128)} %tok_hbm.3, s32[16,64]{1,0:T(8,128)} %lab_hbm.3, bf16[1912,16,128]{2,1,0:T(8,128)(2,1)} %bitcast.3, ...), custom_call_target="tpu_custom_call" | custom-call | tf_op jit(solution)/shard_map/step/pallas_call | solution.py:526
  79.4 14.4 %table_grad.1 = (f32[30592,128]{1,0:T(8,128)}, f32[1]{0:T(128)}, f32[128,512]{1,0:T(8,128)}, f32[512,128]{1,0:T(8,128)}) custom-call(s32[16,64]{1,0:T(8,128)} %tok_hbm.3, s32[16,64]{1,0:T(8,128)} %lab_hbm.3, f32[16,8,128]{2,1,0:T(8,128)} %get-tuple-element.14.misc_hbm, bf16[16,64,128]{2,1,0:T(8,128)(2,1)} %get-tuple-element.15.n_hbm, ...), custom_call_target="tpu_custom_call" | custom-call | tf_op jit(solution)/shard_map/table_grad/pallas_call | solution.py:563

commit v7 on v6

--- a/solution.py
+++ b/solution.py
@@ -13,7 +13,7 @@
 MESH = pl.DeviceIdType.MESH
 LANES = 128
 TILE = 16
-HEAD_COLS = 4096
+HEAD_COLS = 7680
 TABLE_ROWS = 2048
 OUT_ROWS = 2048
 GELU_C = math.sqrt(2.0 / math.pi)
@@ -124,12 +124,13 @@
             src_ref=ref, dst_ref=ref, send_sem=down_send.at[way, slot], recv_sem=down_recv.at[slot],
             device_id=(dp, target), device_id_type=MESH)
 
-    def side_copy(which, slot, kind):
+    def side_copy(which, slot, kind, across=False):
         ref = up_all.at[slot, up_part(kind)] if which == 0 else down_all.at[slot, down_part(kind)]
         give = kind == "give"
         return pltpu.make_async_remote_copy(
-            src_ref=ref, dst_ref=ref, send_sem=side_send.at[0 if give else 1, which, slot], recv_sem=side_recv.at[which, slot],
-            device_id=(side, me) if give else (dp, partner), device_id_type=MESH)
+            src_ref=ref, dst_ref=ref, recv_sem=side_recv.at[which, slot],
+            send_sem=side_send.at[0 if give and not across else 1, which, slot],
+            device_id=(side, partner if across else me) if give else (dp, partner), device_id_type=MESH)
 
     sends = []
 
@@ -154,19 +155,32 @@
     lax.fori_loop(0, seq, embed, 0)
     x_now = x_rows[...].astype(BF16)
 
-    def arrived(copy, which, slot, forward):
+    def arrived(copy, which, slot, forward, across=False):
         copy.wait_recv()
         if forward is not None:
             send(forward)
         if paired:
             send(side_copy(which, slot, "give"))
+            if across:
+                send(side_copy(which, slot, "give", across=True))
+
+    def take(distance, onward=True):
+        for which in (0, 1):
+            taken = side_copy(which, slot_at(distance, core), "take")
+            taken.wait_recv()
+            if onward:
+                send(taken)
 
     for t in range(1, half + 1):
         slot_l, slot_r = slot_at(-t, core), slot_at(t, core)
         whole, onward = t < half, t < half - 1
+        if paired and t == half:
+            for k in range(1, half - 1):
+                take(-k)
+                take(k)
         up_l, down_r = up_copy(slot_l, 0, right, "ring"), down_copy(slot_r, 1, left, "ring")
-        arrived(up_l, 0, slot_l, up_l if whole else None)
-        arrived(down_r, 1, slot_r, down_r if whole else None)
+        arrived(up_l, 0, slot_l, up_l if whole else None, across=t == half)
+        arrived(down_r, 1, slot_r, down_r if whole else None, across=t == half)
         if whole:
             down_l, up_r = down_copy(slot_l, 0, right, "ring"), up_copy(slot_r, 1, left, "ring")
             arrived(down_l, 1, slot_l, down_l if onward else None)
@@ -177,11 +191,9 @@
         send(down_copy(slot_r, 2, partner, "ring"))
 
     if paired:
-        for t in [d for k in range(1, half) for d in (-k, k)] + [half]:
-            for which in (0, 1):
-                taken = side_copy(which, slot_at(t, core), "take")
-                taken.wait_recv()
-                send(taken)
+        take(1 - half)
+        take(half - 1)
+        take(half, onward=False)
 
     for t in range(n_chip):
         slot = slot_at(t, 1 - core)

time: 94 us -> 92.8 us (0.987)
  Pallas kernels: 93.2 us -> 92.1 us
    pallas_call x1, Pallas kernels: 78.8 us -> 77.6 us  [device_fn(): pl.pallas_call(functools.partial(step_kernel, n_stage, mesh.shape['dp'],...]
where the time goes in v7:
time: 92.8 us; the launch traced here: 92.7 us
  Pallas kernels  92.1 us (99%)
    pallas_call x1, Pallas kernels, device_fn(): pl.pallas_call(functools.partial(step_kernel, n_stage, mesh.shape['dp'],...  77.6 us
    pallas_call x1, Pallas kernels, device_fn(): pl.pallas_call(table_kernel, name='table_grad', out_shape=(jax.ShapeDtype...  14.4 us

profile of v7, /device:TPU:21, one launch (start us, length us, event | category | flops | bytes accessed | tf_op | source)
XLA Modules:
  0.0 92.7 jit_solution(11537724616991834240)
XLA Ops:
  0.6 77.6 %step.1 = (bf16[16,64,128]{2,1,0:T(8,128)(2,1)}, bf16[16,64,128]{2,1,0:T(8,128)(2,1)}, bf16[16,64,128]{2,1,0:T(8,128)(2,1)}, bf16[16,64,128]{2,1,0:T(8,128)(2,1)...) custom-call(s32[16,64]{1,0:T(8,128)} %tok_hbm.3, s32[16,64]{1,0:T(8,128)} %lab_hbm.3, bf16[1912,16,128]{2,1,0:T(8,128)(2,1)} %bitcast.3, ...), custom_call_target="tpu_custom_call" | custom-call | tf_op jit(solution)/shard_map/step/pallas_call | solution.py:538
  78.3 14.4 %table_grad.1 = (f32[30592,128]{1,0:T(8,128)}, f32[1]{0:T(128)}, f32[128,512]{1,0:T(8,128)}, f32[512,128]{1,0:T(8,128)}) custom-call(s32[16,64]{1,0:T(8,128)} %tok_hbm.3, s32[16,64]{1,0:T(8,128)} %lab_hbm.3, f32[16,8,128]{2,1,0:T(8,128)} %get-tuple-element.14.misc_hbm, bf16[16,64,128]{2,1,0:T(8,128)(2,1)} %get-tuple-element.15.n_hbm, ...), custom_call_target="tpu_custom_call" | custom-call | tf_op jit(solution)/shard_map/table_grad/pallas_call | solution.py:575

commit v8 on v7

--- a/solution.py
+++ b/solution.py
@@ -94,42 +94,38 @@
     parity = lax.rem(dp, 2)
     up_rows, down_rows = up_all.shape[1], down_all.shape[1]
 
-    def up_part(kind):
-        left_out = up_rows // 64 * 16
-        if kind == "whole" or not paired:
-            return pl.ds(0, up_rows)
-        if kind == "ring":
-            return pl.ds(pl.multiple_of(parity * left_out, 16), up_rows - left_out)
-        mine = parity if kind == "give" else 1 - parity
-        return pl.ds(pl.multiple_of(mine * (up_rows - left_out), 16), left_out)
-
-    def down_part(kind):
-        left_out = down_rows * 5 // 256 * 16
-        if kind == "whole" or not paired:
-            return pl.ds(0, down_rows)
-        if kind == "ring":
-            return pl.ds(pl.multiple_of(parity * left_out, 16), down_rows - left_out)
-        mine = parity if kind == "give" else 1 - parity
-        return pl.ds(pl.multiple_of(mine * (down_rows - left_out), 16), left_out)
-
-    def up_copy(slot, way, target, kind):
-        ref = up_all.at[slot, up_part(kind)]
+    def part(height, left_out, kind, piece):
+        first, size = 0, height
+        if paired and kind == "ring":
+            first, size = parity * left_out, height - left_out
+        elif paired and kind != "whole":
+            first, size = (parity if kind == "give" else 1 - parity) * (height - left_out), left_out
+        return pl.ds(pl.multiple_of(first + piece * (size // 2), 16), size // 2)
+
+    def up_part(kind, piece):
+        return part(up_rows, up_rows // 64 * 16, kind, piece)
+
+    def down_part(kind, piece):
+        return part(down_rows, down_rows * 5 // 256 * 16, kind, piece)
+
+    def up_copy(slot, way, target, kind, piece):
+        ref = up_all.at[slot, up_part(kind, piece)]
         return pltpu.make_async_remote_copy(
-            src_ref=ref, dst_ref=ref, send_sem=up_send.at[way, slot], recv_sem=up_recv.at[slot],
+            src_ref=ref, dst_ref=ref, send_sem=up_send.at[way, piece, slot], recv_sem=up_recv.at[piece, slot],
             device_id=(dp, target), device_id_type=MESH)
 
-    def down_copy(slot, way, target, kind):
-        ref = down_all.at[slot, down_part(kind)]
+    def down_copy(slot, way, target, kind, piece):
+        ref = down_all.at[slot, down_part(kind, piece)]
         return pltpu.make_async_remote_copy(
-            src_ref=ref, dst_ref=ref, send_sem=down_send.at[way, slot], recv_sem=down_recv.at[slot],
+            src_ref=ref, dst_ref=ref, send_sem=down_send.at[way, piece, slot], recv_sem=down_recv.at[piece, slot],
             device_id=(dp, target), device_id_type=MESH)
 
-    def side_copy(which, slot, kind, across=False):
-        ref = up_all.at[slot, up_part(kind)] if which == 0 else down_all.at[slot, down_part(kind)]
+    def side_copy(which, slot, kind, piece, across=False):
+        ref = up_all.at[slot, up_part(kind, piece)] if which == 0 else down_all.at[slot, down_part(kind, piece)]
         give = kind == "give"
         return pltpu.make_async_remote_copy(
-            src_ref=ref, dst_ref=ref, recv_sem=side_recv.at[which, slot],
-            send_sem=side_send.at[0 if give and not across else 1, which, slot],
+            src_ref=ref, dst_ref=ref, recv_sem=side_recv.at[which, piece, slot],
+            send_sem=side_send.at[0 if give and not across else 1, which, piece, slot],
             device_id=(side, partner if across else me) if give else (dp, partner), device_id_type=MESH)
 
     sends = []
@@ -140,7 +136,8 @@
 
     for way, target, kind in ((0, right, "ring"), (1, left, "ring"), (2, partner, "whole")):
         for copy in (down_copy, up_copy) if way == 1 else (up_copy, down_copy):
-            send(copy(me, way, target, kind))
+            for piece in (0, 1):
+                send(copy(me, way, target, kind, piece))
 
     table_copy.wait()
     row_iota = lax.broadcasted_iota(jnp.int32, (TILE, dim), 0)
@@ -155,40 +152,39 @@
     lax.fori_loop(0, seq, embed, 0)
     x_now = x_rows[...].astype(BF16)
 
-    def arrived(copy, which, slot, forward, across=False):
+    def arrived(which, slot, way, onward, piece, across=False):
+        target = (right, left)[way]
+        copy = (up_copy, down_copy)[which](slot, way, target, "ring", piece)
         copy.wait_recv()
-        if forward is not None:
-            send(forward)
-        if paired:
-            send(side_copy(which, slot, "give"))
+        if onward:
+            send(copy)
+        for given in (0, 1) if paired and piece == 1 else ():
+            send(side_copy(which, slot, "give", given))
             if across:
-                send(side_copy(which, slot, "give", across=True))
+                send(side_copy(which, slot, "give", given, across=True))
+        send((up_copy, down_copy)[which](slot, 2, partner, "ring", piece))
 
     def take(distance, onward=True):
         for which in (0, 1):
-            taken = side_copy(which, slot_at(distance, core), "take")
-            taken.wait_recv()
-            if onward:
-                send(taken)
+            for piece in (0, 1):
+                taken = side_copy(which, slot_at(distance, core), "take", piece)
+                taken.wait_recv()
+                if onward:
+                    send(taken)
 
     for t in range(1, half + 1):
         slot_l, slot_r = slot_at(-t, core), slot_at(t, core)
-        whole, onward = t < half, t < half - 1
         if paired and t == half:
             for k in range(1, half - 1):
                 take(-k)
                 take(k)
-        up_l, down_r = up_copy(slot_l, 0, right, "ring"), down_copy(slot_r, 1, left, "ring")
-        arrived(up_l, 0, slot_l, up_l if whole else None, across=t == half)
-        arrived(down_r, 1, slot_r, down_r if whole else None, across=t == half)
-        if whole:
-            down_l, up_r = down_copy(slot_l, 0, right, "ring"), up_copy(slot_r, 1, left, "ring")
-            arrived(down_l, 1, slot_l, down_l if onward else None)
-            arrived(up_r, 0, slot_r, up_r if onward else None)
-            send(down_copy(slot_l, 2, partner, "ring"))
-            send(up_copy(slot_r, 2, partner, "ring"))
-        send(up_copy(slot_l, 2, partner, "ring"))
-        send(down_copy(slot_r, 2, partner, "ring"))
+        for piece in (0, 1):
+            arrived(0, slot_l, 0, t < half, piece, across=t == half)
+            arrived(1, slot_r, 1, t < half, piece, across=t == half)
+        if t < half:
+            for piece in (0, 1):
+                arrived(1, slot_l, 0, t < half - 1, piece)
+                arrived(0, slot_r, 1, t < half - 1, piece)
 
     if paired:
         take(1 - half)
@@ -198,11 +194,12 @@
     for t in range(n_chip):
         slot = slot_at(t, 1 - core)
         kind = "whole" if t == 0 else "ring"
-        up_copy(slot, 2, partner, kind).wait_recv()
-        down_copy(slot, 2, partner, kind).wait_recv()
-        if paired and t > 0:
-            side_copy(0, slot, "take").wait_recv()
-            side_copy(1, slot, "take").wait_recv()
+        for piece in (0, 1):
+            up_copy(slot, 2, partner, kind, piece).wait_recv()
+            down_copy(slot, 2, partner, kind, piece).wait_recv()
+            if paired and t > 0:
+                side_copy(0, slot, "take", piece).wait_recv()
+                side_copy(1, slot, "take", piece).wait_recv()
 
     def forward(s, x_act):
         x_hist[s] = x_act
@@ -562,8 +559,8 @@
                 pltpu.VMEM((n_stage, seq, dim), BF16),
                 pltpu.VMEM((n_stage, seq, dim), BF16),
                 pltpu.VMEM((n_stage, seq, dim), BF16),
-                dma((4,)), dma((5,)), dma, dma((n_stage,)), dma((n_stage,)), dma((3, n_stage)), dma((3, n_stage)),
-                dma((2, n_stage)), dma((2, 2, n_stage)),
+                dma((4,)), dma((5,)), dma, dma((2, n_stage)), dma((2, n_stage)), dma((3, 2, n_stage)), dma((3, 2, n_stage)),
+                dma((2, 2, n_stage)), dma((2, 2, 2, n_stage)),
                 dma((n_stage,)), dma((n_stage,)), dma((n_stage,)), dma((n_stage,)), dma((n_stage,)),
                 dma((n_stage,)), dma((n_stage,)), dma((n_stage,)), dma((n_stage,)), dma((n_stage,)),
                 dma((n_parts,)), dma((n_parts,)), dma((n_parts,)),

time: 92.8 us -> 96.8 us (1.043)
  Pallas kernels: 92.1 us -> 96.1 us
    pallas_call x1, Pallas kernels: 77.6 us -> 81.7 us  [device_fn(): pl.pallas_call(functools.partial(step_kernel, n_stage, mesh.shape['dp'],...]
where the time goes in v8:
time: 96.8 us; the launch traced here: 96.7 us
  Pallas kernels  96.1 us (99%)
    pallas_call x1, Pallas kernels, device_fn(): pl.pallas_call(functools.partial(step_kernel, n_stage, mesh.shape['dp'],...  81.7 us
    pallas_call x1, Pallas kernels, device_fn(): pl.pallas_call(table_kernel, name='table_grad', out_shape=(jax.ShapeDtype...  14.4 us

profile of v8, /device:TPU:21, one launch (start us, length us, event | category | flops | bytes accessed | tf_op | source)
XLA Modules:
  0.0 96.7 jit_solution(1323568389453549841)
XLA Ops:
  0.6 81.7 %step.1 = (bf16[16,64,128]{2,1,0:T(8,128)(2,1)}, bf16[16,64,128]{2,1,0:T(8,128)(2,1)}, bf16[16,64,128]{2,1,0:T(8,128)(2,1)}, bf16[16,64,128]{2,1,0:T(8,128)(2,1)...) custom-call(s32[16,64]{1,0:T(8,128)} %tok_hbm.3, s32[16,64]{1,0:T(8,128)} %lab_hbm.3, bf16[1912,16,128]{2,1,0:T(8,128)(2,1)} %bitcast.3, ...), custom_call_target="tpu_custom_call" | custom-call | tf_op jit(solution)/shard_map/step/pallas_call | solution.py:535
  82.3 14.4 %table_grad.1 = (f32[30592,128]{1,0:T(8,128)}, f32[1]{0:T(128)}, f32[128,512]{1,0:T(8,128)}, f32[512,128]{1,0:T(8,128)}) custom-call(s32[16,64]{1,0:T(8,128)} %tok_hbm.3, s32[16,64]{1,0:T(8,128)} %lab_hbm.3, f32[16,8,128]{2,1,0:T(8,128)} %get-tuple-element.14.misc_hbm, bf16[16,64,128]{2,1,0:T(8,128)(2,1)} %get-tuple-element.15.n_hbm, ...), custom_call_target="tpu_custom_call" | custom-call | tf_op jit(solution)/shard_map/table_grad/pallas_call | solution.py:572
